TPU v7x, 32 devices: a whole 2x2x4 slice. The times are simulated.
32 devices in a mesh: dp: 4 (over y, x), ctx: 8 (over z, core).
Axes of the slice: x: 2, y: 2, z: 4, core: 2. Of those that a mesh axis runs over, the one named last changes fastest.
Arguments:
- tokens: bfloat16 [4, 1024, 1024], P('dp', 'ctx'), may hold values from -50 to 50
- cotangent: bfloat16 [4, 1024, 1024], P('dp', 'ctx'), may hold values from -6 to 6
- weights: float32 [12596224], P('ctx'), may hold values from -5 to 5, as said below
- first_moment: float32 [12596224], P('ctx'), may hold values from -48 to 48
- second_moment: float32 [12596224], P('ctx'), may hold values from 100 to 3000
Outputs:
- layer_out: bfloat16 [4, 1024, 1024], P('dp', 'ctx')
- token_grads: float32 [4, 1024, 1024], P('dp', 'ctx')
- weight_grads: float32 [12596224], P('ctx')
- new_weights: float32 [12596224], P('ctx')
- new_first: float32 [12596224], P('ctx')
- new_second: float32 [12596224], P('ctx')
Inputs may be any that keep to these rules, and one draw needn't show every extreme that they name: `weights`: the parameters laid end to end in the order of the first step.
All inputs are finite; a program needn't handle non-finite values.
Results may differ from a plain program's by a relative error of at most 0.012.
Values may be sent and summed in bfloat16 or wider, within the bound.
A program may use at most 320 MiB of HBM per device.

v0:
```python
from functools import partial

import jax
import jax.numpy as jnp
from jax import lax
from jax.sharding import PartitionSpec as P

D = 1024
FF = 4096
HEADS = 16
HEAD_DIM = 64
ROT = 16
STEP = 3


BETA_ONE = 0.9
BETA_TWO = 0.95
LEARN_RATE = 0.004
DECAY_RATE = 0.1
EPSILON = 1e-08


def unpack(flat_params):
    lengths = [D * 3 * D, D * D, D * FF, FF * D, 9 * D, FF]
    dims_list = [(D, 3 * D), (D, D), (D, FF), (FF, D), (9, D), (FF,)]
    pieces = []
    offset = 0
    for length, dims_of in zip(lengths, dims_list):
        pieces.append(lax.slice_in_dim(flat_params, offset, offset + length).reshape(dims_of))
        offset += length
    return pieces


def rotary_tables(positions):
    halfrot = ROT // 2
    frequency = 10000.0 ** (-2.0 * jnp.arange(halfrot, dtype=jnp.float32) / ROT)
    angles = positions.astype(jnp.float32)[:, None] * frequency[None, :]
    return (jnp.cos(angles)[:, None, :], jnp.sin(angles)[:, None, :])


def rotate(head_vals, cosine, sine_table):
    halfrot = ROT // 2
    first_half = head_vals[..., :halfrot]
    second_half = head_vals[..., halfrot:ROT]
    return jnp.concatenate(
        [
            first_half * cosine - second_half * sine_table,
            second_half * cosine + first_half * sine_table,
            head_vals[..., ROT:],
        ],
        axis=-1,
    )


def norm_parts(values, gain_row, shift_row):
    average = jnp.mean(values, axis=-1, keepdims=True)
    centred = values - average
    spread = jnp.mean(centred * centred, axis=-1, keepdims=True)
    inverse = lax.rsqrt(spread + 1e-05)
    normed = centred * inverse
    return (normed * gain_row + shift_row, normed, inverse)


def norm_back(grad_norm, normed, inverse, gain_row):
    scaled = grad_norm * gain_row
    inner_term = (
        scaled
        - jnp.mean(scaled, axis=-1, keepdims=True)
        - normed * jnp.mean(scaled * normed, axis=-1, keepdims=True)
    )
    return (inverse * inner_term, jnp.sum(grad_norm * normed, axis=0), jnp.sum(grad_norm, axis=0))


def contract_rows(left_op, right_op):
    return lax.dot_general(
        left_op, right_op, (((0,), (0,)), ((), ())), preferred_element_type=jnp.float32
    )


def contract_cols(left_op, right_op):
    return lax.dot_general(
        left_op, right_op, (((1,), (1,)), ((), ())), preferred_element_type=jnp.float32
    )


def block_scores(queries, piece_k, query_pos, key_pos):
    scores = jnp.einsum("qhd,khd->hqk", queries, piece_k, preferred_element_type=jnp.float32)
    return jnp.where(key_pos[None, None, :] <= query_pos[None, :, None], scores, -1e30)


def local(tokens, cotangent, weights, first_moment, second_moment):
    own_index = lax.axis_index("ctx")
    ctx_count = lax.axis_size("ctx")
    data_count = lax.axis_size("dp")
    local_rows = tokens.shape[1]
    gathered = lax.all_gather(weights.astype(jnp.bfloat16), "ctx", axis=0, tiled=True)
    weight_qkv, weight_out, weight_up, weight_down, vectors, bias_up = unpack(gathered)
    small_params = vectors.astype(jnp.float32)
    up_bias = bias_up.astype(jnp.float32)
    inputs = tokens[0].astype(jnp.float32)
    grad_out = cotangent[0]
    query_pos = own_index * local_rows + jnp.arange(local_rows, dtype=jnp.int32)
    cosine, sine_table = rotary_tables(query_pos)
    norm_one, normed_one, inverse_one = norm_parts(inputs, small_params[0], small_params[1])
    norm_two, normed_two, inverse_two = norm_parts(inputs, small_params[2], small_params[3])
    one_low = norm_one.astype(jnp.bfloat16)
    two_low = norm_two.astype(jnp.bfloat16)
    joined_qkv = jnp.dot(one_low, weight_qkv, preferred_element_type=jnp.float32) + small_params[
        4:7
    ].reshape(-1)
    query_h = joined_qkv[:, :D].reshape(local_rows, HEADS, HEAD_DIM)
    key_h = joined_qkv[:, D : 2 * D].reshape(local_rows, HEADS, HEAD_DIM)
    queries = (rotate(query_h, cosine, sine_table) * 0.125).astype(jnp.bfloat16)
    keys_local = rotate(key_h, cosine, sine_table).astype(jnp.bfloat16).reshape(local_rows, D)
    values_local = joined_qkv[:, 2 * D :].astype(jnp.bfloat16)
    keys_all, values_all = (
        lax.all_gather(keys_local, "ctx", axis=0, tiled=True),
        lax.all_gather(values_local, "ctx", axis=0, tiled=True),
    )
    kblock = 2 * local_rows
    block_count = own_index // 2 + 1

    def key_block(source, block_idx):
        first_row = block_idx * kblock
        piece_k = lax.dynamic_slice_in_dim(source[0], first_row, kblock, 0).reshape(
            kblock, HEADS, HEAD_DIM
        )
        piece_v = lax.dynamic_slice_in_dim(source[1], first_row, kblock, 0).reshape(
            kblock, HEADS, HEAD_DIM
        )
        key_pos = first_row + jnp.arange(kblock, dtype=jnp.int32)
        return (piece_k, piece_v, key_pos)

    def stats_step(block_idx, state_pair):
        row_top, row_sum = state_pair
        piece_k, piece_v, key_pos = key_block((keys_all, values_all), block_idx)
        scores = block_scores(queries, piece_k, query_pos, key_pos)
        new_top = jnp.maximum(row_top, jnp.max(scores, axis=-1))
        row_sum = row_sum * jnp.exp(row_top - new_top) + jnp.sum(
            jnp.exp(scores - new_top[..., None]), axis=-1
        )
        return (new_top, row_sum)

    start_top = jnp.full((HEADS, local_rows), -1e30, jnp.float32)
    row_top, row_sum = lax.fori_loop(
        0, block_count, stats_step, (start_top, jnp.zeros((HEADS, local_rows), jnp.float32))
    )
    log_total = row_top + jnp.log(row_sum)

    def output_step(block_idx, running):
        piece_k, piece_v, key_pos = key_block((keys_all, values_all), block_idx)
        scores = block_scores(queries, piece_k, query_pos, key_pos)
        probability = jnp.exp(scores - log_total[..., None]).astype(jnp.bfloat16)
        return running + jnp.einsum(
            "hqk,khd->qhd", probability, piece_v, preferred_element_type=jnp.float32
        )

    attended = lax.fori_loop(
        0, block_count, output_step, jnp.zeros((local_rows, HEADS, HEAD_DIM), jnp.float32)
    )
    mixed = attended.reshape(local_rows, D).astype(jnp.bfloat16)
    branch_attn = jnp.dot(mixed, weight_out, preferred_element_type=jnp.float32) + small_params[7]
    upward = jnp.dot(two_low, weight_up, preferred_element_type=jnp.float32) + up_bias
    activated, gelu_pull = jax.vjp(partial(jax.nn.gelu, approximate=False), upward)
    hidden = activated.astype(jnp.bfloat16)
    branch_mlp = jnp.dot(hidden, weight_down, preferred_element_type=jnp.float32) + small_params[8]
    layer_out = (inputs + branch_attn + branch_mlp).astype(jnp.bfloat16)
    grad_float = grad_out.astype(jnp.float32)
    grad_wout = contract_rows(mixed, grad_out)
    grad_wdown = contract_rows(hidden, grad_out)
    grad_bias = jnp.sum(grad_float, axis=0)
    d_hidden = contract_cols(grad_out, weight_down)
    d_upward = gelu_pull(d_hidden)[0].astype(jnp.bfloat16)
    grad_upbias = jnp.sum(d_upward.astype(jnp.float32), axis=0)
    grad_wup = contract_rows(two_low, d_upward)
    d_norm_two = contract_cols(d_upward, weight_up)
    d_mixed = contract_cols(grad_out, weight_out).astype(jnp.bfloat16)
    d_heads = d_mixed.reshape(local_rows, HEADS, HEAD_DIM)
    kv_back = (keys_all, values_all)

    def delta_step(block_idx, running):
        piece_k, piece_v, key_pos = key_block(kv_back, block_idx)
        scores = block_scores(queries, piece_k, query_pos, key_pos)
        probability = jnp.exp(scores - log_total[..., None])
        d_probs = jnp.einsum("qhd,khd->hqk", d_heads, piece_v, preferred_element_type=jnp.float32)
        return running + jnp.sum(probability * d_probs, axis=-1)

    row_delta = lax.fori_loop(
        0, block_count, delta_step, jnp.zeros((HEADS, local_rows), jnp.float32)
    )

    def query_step(block_idx, running):
        piece_k, piece_v, key_pos = key_block(kv_back, block_idx)
        scores = block_scores(queries, piece_k, query_pos, key_pos)
        probability = jnp.exp(scores - log_total[..., None])
        d_probs = jnp.einsum("qhd,khd->hqk", d_heads, piece_v, preferred_element_type=jnp.float32)
        d_scores = (probability * (d_probs - row_delta[..., None])).astype(jnp.bfloat16)
        return running + jnp.einsum(
            "hqk,khd->qhd", d_scores, piece_k, preferred_element_type=jnp.float32
        )

    d_queries = lax.fori_loop(
        0, block_count, query_step, jnp.zeros((local_rows, HEADS, HEAD_DIM), jnp.float32)
    )
    all_queries, all_dheads = (
        lax.all_gather(queries, "ctx", axis=0, tiled=True),
        lax.all_gather(d_heads, "ctx", axis=0, tiled=True),
    )
    all_lse, all_delta = (
        lax.all_gather(log_total.T, "ctx", axis=0, tiled=True),
        lax.all_gather(row_delta.T, "ctx", axis=0, tiled=True),
    )
    own_keys = keys_local.reshape(local_rows, HEADS, HEAD_DIM)
    own_values = values_local.reshape(local_rows, HEADS, HEAD_DIM)

    def owner_step(block_idx, running):
        first_row = block_idx * kblock
        block_q = lax.dynamic_slice_in_dim(all_queries, first_row, kblock, 0)
        block_do = lax.dynamic_slice_in_dim(all_dheads, first_row, kblock, 0)
        block_lse = lax.dynamic_slice_in_dim(all_lse, first_row, kblock, 0).T
        block_delta = lax.dynamic_slice_in_dim(all_delta, first_row, kblock, 0).T
        block_pos = first_row + jnp.arange(kblock, dtype=jnp.int32)
        scores = block_scores(block_q, own_keys, block_pos, query_pos)
        probability = jnp.exp(scores - block_lse[..., None])
        d_probs = jnp.einsum(
            "qhd,khd->hqk", block_do, own_values, preferred_element_type=jnp.float32
        )
        d_scores = (probability * (d_probs - block_delta[..., None])).astype(jnp.bfloat16)
        d_keys = jnp.einsum("hqk,qhd->khd", d_scores, block_q, preferred_element_type=jnp.float32)
        d_values = jnp.einsum(
            "hqk,qhd->khd",
            probability.astype(jnp.bfloat16),
            block_do,
            preferred_element_type=jnp.float32,
        )
        return (running[0] + d_keys, running[1] + d_values)

    empty_grad = jnp.zeros((local_rows, HEADS, HEAD_DIM), jnp.float32)
    owner_keys, owner_values = lax.fori_loop(
        own_index // 2, ctx_count // 2, owner_step, (empty_grad, empty_grad)
    )
    key_terms = jnp.concatenate(
        [owner_keys.reshape(local_rows, D), owner_values.reshape(local_rows, D)], axis=1
    )
    d_query = rotate(d_queries * 0.125, cosine, -sine_table).reshape(local_rows, D)
    d_key = rotate(
        key_terms[:, :D].reshape(local_rows, HEADS, HEAD_DIM), cosine, -sine_table
    ).reshape(local_rows, D)
    d_joined = jnp.concatenate([d_query, d_key, key_terms[:, D:]], axis=1).astype(jnp.bfloat16)
    grad_qkvbias = jnp.sum(d_joined.astype(jnp.float32), axis=0)
    grad_wqkv = contract_rows(one_low, d_joined)
    d_norm_one = contract_cols(d_joined, weight_qkv)
    d_in_one, grad_gain_one, grad_shift_one = norm_back(
        d_norm_one, normed_one, inverse_one, small_params[0]
    )
    d_in_two, grad_gain_two, grad_shift_two = norm_back(
        d_norm_two, normed_two, inverse_two, small_params[2]
    )
    token_grads = grad_float + d_in_one + d_in_two
    grad_vectors = jnp.stack(
        [
            grad_gain_one,
            grad_shift_one,
            grad_gain_two,
            grad_shift_two,
            grad_qkvbias[:D],
            grad_qkvbias[D : 2 * D],
            grad_qkvbias[2 * D :],
            grad_bias,
            grad_bias,
        ]
    )
    local_grad = jnp.concatenate(
        [
            grad_wqkv.reshape(-1),
            grad_wout.reshape(-1),
            grad_wup.reshape(-1),
            grad_wdown.reshape(-1),
            grad_vectors.reshape(-1),
            grad_upbias,
        ]
    )
    share_len = local_grad.shape[0] // (ctx_count * data_count)
    arranged = (
        local_grad.reshape(ctx_count, data_count, share_len)
        .transpose(1, 0, 2)
        .reshape(ctx_count * data_count, share_len)
    )
    my_share = lax.psum_scatter(arranged, ("dp", "ctx"), scatter_dimension=0, tiled=True)
    grad_shard = lax.all_gather(my_share, "dp", axis=0, tiled=True).reshape(-1)
    new_first = BETA_ONE * first_moment + (1.0 - BETA_ONE) * grad_shard
    new_second = BETA_TWO * second_moment + (1.0 - BETA_TWO) * grad_shard * grad_shard
    corrected_m = new_first / (1.0 - BETA_ONE**STEP)
    corrected_v = new_second / (1.0 - BETA_TWO**STEP)
    new_weights = weights - LEARN_RATE * (
        corrected_m / (jnp.sqrt(corrected_v) + EPSILON) + DECAY_RATE * weights
    )
    return (layer_out[None], token_grads[None], grad_shard, new_weights, new_first, new_second)


def solution(mesh):
    return jax.shard_map(
        local,
        mesh=mesh,
        in_specs=(P("dp", "ctx", None), P("dp", "ctx", None), P("ctx"), P("ctx"), P("ctx")),
        out_specs=(
            P("dp", "ctx", None),
            P("dp", "ctx", None),
            P("ctx"),
            P("ctx"),
            P("ctx"),
            P("ctx"),
        ),
        check_vma=False,
    )
```

profile of v0, /device:TPU:15, one launch (start us, length us, event | category | flops | bytes accessed | tf_op | source)
XLA Modules:
  0.0 1952.6 jit_solution(17040296698921753126)
XLA Ops:
  10.2 36.8 %reshape.502 = bf16[1,1,1574528]{2,1,0:T(2,128)(2,1)} reshape(bf16[1574528]{0:T(1024)(128)(2,1)S(1)} %convert_element_type.95) | data formatting | bytes 6298112
  49.1 424.7 %all-gather.17.cloned.1.call-done = bf16[8,1,1574528]{2,1,0:T(2,128)(2,1)} async-done(((bf16[1,1,1574528]{2,1,0:T(2,128)(2,1)}), bf16[8,1,1574528]{2,1,0:T(2,128)(2,1)}) %all-gather.17.cloned.1.call-update) | async-done | bytes 25192464 | tf_op jit(solution)/shard_map/all_gather | solution.py:96
  473.8 136.5 %reduce.1 = bf16[8,1574528]{1,0:T(8,128)(2,1)} reduce(bf16[8,1,1574528]{2,1,0:T(2,128)(2,1)} %all-gather.17.cloned.1.call-done, bf16[]{:T(256)} %constant.191), dimensions={1}, to_apply=%all-gather.reduce_sub_computation | reduce | bytes 50384896 | tf_op jit(solution)/shard_map/all_gather | solution.py:96
  610.3 54.7 %reshape.503 = bf16[12596224]{0:T(1024)(128)(2,1)} reshape(bf16[8,1574528]{1,0:T(8,128)(2,1)} %reduce.1) | data formatting | bytes 50384896
  665.7 6.4 slice.169
  672.8 10.3 reshape.485
  689.7 11.4 fusion.137
  702.9 13.4 slice.155
  716.3 13.5 reshape.488
  743.1 10.8 convert_reduce_fusion
  756.5 7.2 copy.59
  763.7 6.3 convolution_bitcast_fusion.1
  769.9 8.1 copy.60
  786.2 18.9 all_gather.28
  808.0 7.2 while.61
  815.2 21.1 %all_gather.30 = f32[1024,16]{0,1:T(8,128)S(1)} all-gather(f32[128,16]{0,1:T(8,128)S(1)} %bitcast.339), channel_id=1, replica_groups=mesh['dp'=4,'ctx'=8] {'ctx'}, dimensions={0}, use_global_device_ids=true | all-gather | bytes 73728 | tf_op jit(solution)/shard_map/all_gather | solution.py:211
  837.2 23.0 %while.63 = (s32[]{:T(128)}, f32[128,16,64]{0,2,1:T(8,128)}, f32[128,16,64]{0,2,1:T(8,128)S(1)}, bf16[1024,16,64]{0,2,1:T(8,128)(2,1)}, bf16[128,16,64]{0,2,1:T(...) while((s32[]{:T(128)}, f32[128,16,64]{0,2,1:T(8,128)}, ...), condition=%wide.region_14.15_spmd.clone, body=%wide.region_13.14_spmd.clone.sunk | while | flops 272925056 | bytes 11227343 | solution.py:239
  861.8 9.6 while.62
  874.7 6.4 convolution_bitcast_fusion.3
  891.8 12.1 copy.57
  903.8 10.0 constant_dynamic-update-slice_fusion.5
  923.4 13.2 constant_dynamic-update-slice_fusion.3
  938.8 6.2 constant_dynamic-update-slice_fusion.2
  946.2 67.7 %reshape.499 = f32[8,4,393632]{2,1,0:T(4,128)} reshape(f32[12596224]{0:T(1024)} %constant_dynamic-update-slice_fusion) | data formatting | bytes 100769792 | tf_op jit(solution)/shard_map/reshape | solution.py:285
  1013.9 37.6 %copy.62 = f32[4,8,393632]{2,1,0:T(8,128)} copy(f32[4,8,393632]{2,0,1:T(4,128)} %bitcast.306) | data formatting | bytes 100769792 | tf_op jit(solution)/shard_map/transpose | solution.py:286
  1051.6 720.3 %all-reduce.3.cloned.1.call-done = f32[32,393632]{1,0:T(8,128)} async-done(((f32[32,393632]{1,0:T(8,128)}), f32[32,393632]{1,0:T(8,128)}) %all-reduce.3.cloned.1.call-update) | async-done | bytes 50384912
  1771.9 6.4 dynamic-slice_bitcast_fusion.2
  1778.4 8.1 convolution_add_fusion.3
  1787.7 60.5 %all-gather.19.cloned.1.call-done = f32[4,1,393632]{2,1,0:T(1,128)} async-done(((f32[1,1,393632]{2,1,0:T(1,128)}), f32[4,1,393632]{2,1,0:T(1,128)}) %all-gather.19.cloned.1.call-update) | async-done | bytes 6298128 | tf_op jit(solution)/shard_map/all_gather | solution.py:290
  1848.1 70.5 %reduce.2 = f32[4,393632]{1,0:T(4,128)} reduce(f32[4,1,393632]{2,1,0:T(1,128)} %all-gather.19.cloned.1.call-done, f32[]{:T(128)} %constant.192), dimensions={1}, to_apply=%all-gather.1.reduce_sub_computation | reduce | bytes 12596228 | tf_op jit(solution)/shard_map/all_gather | solution.py:290
  1918.6 10.0 reshape.501
  1928.6 16.9 multiply_subtract_fusion
  (232 shorter events, 119.8 us)
Async XLA Ops:
  7.2 466.6 %all-gather.17.cloned.1.call-start = ((), (), s32[]{:S(2)}) async-start(), calls=%async_computation.4 | async-start | bytes 56683008 | tf_op jit(solution)/shard_map/all_gather | solution.py:96
  47.1 734.7 %all-gather.11.cloned.1.call-start = ((), (), s32[]{:S(2)}) async-start(), calls=%async_computation.1 | async-start | bytes 2359296 | tf_op jit(solution)/shard_map/all_gather | solution.py:117
  48.1 634.9 %copy-start.17 = (f32[128]{0:T(128)}, f32[128]{0:T(128)S(1)}, u32[]{:S(2)}) copy-start(f32[128]{0:T(128)S(1)} %broadcast_multiply_fusion.5) | copy-start | bytes 1540
  48.4 634.7 %copy-start.20 = (f32[128]{0:T(128)}, f32[128]{0:T(128)S(1)}, u32[]{:S(2)}) copy-start(f32[128]{0:T(128)S(1)} %add_rsqrt_fusion) | copy-start | bytes 1540
  49.1 639.0 %copy-start.14 = (f32[128,8]{0,1:T(8,128)}, f32[128,8]{0,1:T(8,128)S(1)}, u32[]{:S(2)}) copy-start(f32[128,8]{0,1:T(8,128)S(1)} %get-tuple-element.614) | copy-start | bytes 12292
  49.1 639.0 %copy-start.23 = (f32[128,8]{0,1:T(8,128)}, f32[128,8]{0,1:T(8,128)S(1)}, u32[]{:S(2)}) copy-start(f32[128,8]{0,1:T(8,128)S(1)} %get-tuple-element.613) | copy-start | bytes 12292
  665.7 7.0 copy-start.13
  672.8 10.3 slice-start.7
  688.9 116.2 %all-gather.9.cloned.1.call-start = ((), (), s32[]{:S(2)}) async-start(), calls=%async_computation | async-start | bytes 2359296 | tf_op jit(solution)/shard_map/all_gather | solution.py:118
  689.7 146.6 %all-gather.13.cloned.1.call-start = ((), (), s32[]{:S(2)}) async-start(), calls=%async_computation.2 | async-start | bytes 2359296 | tf_op jit(solution)/shard_map/all_gather | solution.py:206
  716.3 14.8 slice-start.2
  738.2 98.1 %all-gather.15.cloned.1.call-start = ((), (), s32[]{:S(2)}) async-start(), calls=%async_computation.3 | async-start | bytes 2359296 | tf_op jit(solution)/shard_map/all_gather | solution.py:207
  743.1 20.5 %copy-start.10 = (f32[128,4096]{1,0:T(8,128)}, f32[128,4096]{1,0:T(8,128)S(1)}, u32[]{:S(2)}) copy-start(f32[128,4096]{1,0:T(8,128)S(1)} %convolution_add_fusion) | copy-start | bytes 6291460
  756.4 21.5 %slice-start = ((s8[8388608]{0:T(1024)(128)(4,1)}), s8[4194304]{0:T(1024)(128)(4,1)S(1)}, s32[]{:S(2)}) async-start(s8[8388608]{0:T(1024)(128)(4,1)} %bitcast.309), calls=%async_computation.7 | async-start | bytes 8388608
  763.6 14.3 slice-start.1
  781.7 990.2 %all-reduce.3.cloned.1.call-start = ((), (), s32[]{:S(2)}) async-start(), calls=%async_computation.6 | async-start | bytes 100794368
  808.0 29.3 %copy-start.5 = (bf16[128,16,64]{0,2,1:T(8,128)(2,1)S(1)}, bf16[128,16,64]{0,2,1:T(8,128)(2,1)}, u32[]{:S(2)}) copy-start(bf16[128,16,64]{0,2,1:T(8,128)(2,1)} %maximum_convert_fusion) | copy-start | bytes 786436
  815.2 22.0 %copy-start.1 = (bf16[1024,1024]{0,1:T(8,128)(2,1)}, bf16[1024,1024]{0,1:T(8,128)(2,1)S(1)}, u32[]{:S(2)}) copy-start(bf16[1024,1024]{0,1:T(8,128)(2,1)S(1)} %get-tuple-element.1124) | copy-start | bytes 6291460
  861.8 11.8 copy-start.16
  861.8 11.8 copy-start.26
  881.4 5.1 copy-start.12
  903.8 10.0 copy-start.7
  918.8 17.8 slice-start.3
  923.4 13.2 slice-start.4
  923.4 14.0 slice-start.5
  923.4 15.3 slice-start.6
  938.8 6.9 copy-start.27
  1051.5 796.6 %all-gather.19.cloned.1.call-start = ((), (), s32[]{:S(2)}) async-start(), calls=%async_computation.5 | async-start | bytes 7874560 | tf_op jit(solution)/shard_map/all_gather | solution.py:290
  1051.6 726.8 %copy-start.11 = (f32[128,4096]{1,0:T(8,128)S(1)}, f32[128,4096]{1,0:T(8,128)}, u32[]{:S(2)}) copy-start(f32[128,4096]{1,0:T(8,128)} %copy-done.10) | copy-start | bytes 6291460
  1051.6 726.8 %copy-start.28 = (f32[1024]{0:T(1024)S(1)}, f32[1024]{0:T(1024)}, u32[]{:S(2)}) copy-start(f32[1024]{0:T(1024)} %get-tuple-element.602) | copy-start | bytes 12292
  1778.4 8.1 copy-start.4
  1778.4 8.1 copy-start.25
  (12 other events, 37.4 us)
Sparse Core Ops, SparseCore 0:
  47.2 426.5 all-gather.16
  689.0 30.4 all-gather.10
  721.7 29.1 all-gather.8
  752.9 28.9 all-gather.12
  783.4 30.2 all-gather.14
  1051.6 720.2 all-reduce.2
  1778.5 69.6 all-gather.18
where the time goes:
time: 1960 us; the launch traced here: 1950 us
  waiting for transfers between devices  1210 us (62%)
  local copies, waits for them, and re-layouts  361 us (18%)
  other arithmetic  237 us (12%)
  matrix products  92.1 us (5%)
  blocking collectives  40 us (2%)
    unnamed x8, waiting for transfers between devices  720 us
    all_gather x1, waiting for transfers between devices, local(): lax.all_gather(weights.astype(jnp.bfloat16), 'ctx', axis=0, tiled=True)  425 us
    unnamed x83, local copies, waits for them, and re-layouts  170 us
    all_gather x1, other arithmetic, local(): lax.all_gather(weights.astype(jnp.bfloat16), 'ctx', axis=0, tiled=True)  136 us
    all_gather x1, other arithmetic, local(): grad_shard = lax.all_gather(my_share, 'dp', axis=0, tiled=True).reshape(-1)  70.5 us
    reshape x1, local copies, waits for them, and re-layouts, local(): local_grad.reshape(ctx_count, data_count, share_len).transpose(1, 0, 2)  67.7 us
    all_gather x1, waiting for transfers between devices, local(): grad_shard = lax.all_gather(my_share, 'dp', axis=0, tiled=True).reshape(-1)  60.5 us
  transfers between devices with their start and end apart: 7, of which 3 were waited for; matrix products, arithmetic and copies ran while one was open for 6% of the time, Pallas kernels for 0%

commit v1 on v0

v1 whole, which is shorter than its diff:
```python
from functools import partial
import math

import numpy as np
import jax
import jax.numpy as jnp
from jax import lax
from jax.experimental import pallas as pl
from jax.experimental.pallas import tpu as pltpu
from jax.sharding import PartitionSpec as P

D = 1024
FF = 4096
HEADS = 16
HEAD_DIM = 64
ROT = 16
STEP = 3
BETA_ONE = 0.9
BETA_TWO = 0.95
LEARN_RATE = 0.004
DECAY_RATE = 0.1
EPSILON = 1e-08

F32 = jnp.float32
BF16 = jnp.bfloat16
MESH = pl.DeviceIdType.MESH
V = 8
CHIPS = V // 2
OWN = 12301
ALI = 12288
VECS = 104
HEAD = 112
RB = 256


class Geo:
    def __init__(self, mesh, tokens):
        self.q = mesh.shape["dp"]
        self.rep = mesh.shape["ctx"] // V
        self.tl = tokens // V
        self.t = tokens
        q = self.q
        self.qr = 512 // q
        self.ho = 128 // q
        self.u2 = 128 // q
        self.u3 = 384 // q
        self.seg = 1536 // q
        self.zr = V * self.seg
        self.ap = 1024 // q
        self.bp = 512 // q
        self.er = 2 * self.ap

    def place(self):
        d = lax.axis_index("dp")
        a = lax.axis_index("ctx")
        return d, a // self.rep, a % self.rep

    def dev(self, e, j, rho):
        return {"dp": e, "ctx": j * self.rep + rho}

    def maps(self):
        q, out = self.q, []
        for e in range(q):
            for i in range(2):
                for s in range(3):
                    out.append((e, self.seg * i + self.qr * s, self.qr, 0, 512 * i + self.qr * e, 128 * s))
            for b in range(8):
                out.append((e, 2 * self.seg + self.ho * b, self.ho, 1, self.ho * e, 128 * b))
            parts = (
                (0, self.u2, 2 * self.seg + self.ap),
                (128, self.u3, 3 * self.seg),
                (512, self.u3, 4 * self.seg),
                (896, self.u2, 5 * self.seg),
            )
            for r0, nr, off in parts:
                for t in range(4):
                    out.append((e, off + nr * t, nr, 2, r0 + nr * e, 128 * t))
            for t in range(4):
                for b in range(8):
                    row = 5 * self.seg + self.bp + self.ap * t + self.ho * b
                    out.append((e, row, self.ho, 3, 128 * t + self.ho * e, 128 * b))
        return out


def dot(a, b):
    return jnp.dot(a, b, preferred_element_type=F32)


def dot_nt(a, b):
    return lax.dot_general(a, b, (((1,), (1,)), ((), ())), preferred_element_type=F32)


def dot_tn(a, b):
    return lax.dot_general(a, b, (((0,), (0,)), ((), ())), preferred_element_type=F32)


def mult(x, n):
    return pl.multiple_of(x, n)


def view(part):
    return part[0].at[part[1]] if isinstance(part, tuple) else part


def rcopy(src, dst, ssem, rsem, dev):
    return pltpu.make_async_remote_copy(
        src_ref=view(src),
        dst_ref=view(dst),
        send_sem=view(ssem),
        recv_sem=view(rsem),
        device_id=dev,
        device_id_type=MESH,
    )


class Sends:
    def __init__(self, ssem, rsem):
        self.ssem, self.rsem, self.used, self.open = ssem, rsem, 0, []

    def slot(self):
        self.used += 1
        return (self.ssem, self.used - 1)

    def send(self, cond, src, dst, rs, dev):
        slot = self.slot()
        make = lambda: rcopy(src, dst, slot, (self.rsem, rs), dev)
        self.when(cond, lambda: make().start())
        self.open.append((cond, lambda: make().wait_send()))

    def copy(self, cond, src, dst):
        slot = self.slot()
        make = lambda: pltpu.make_async_copy(view(src), view(dst), view(slot))
        self.when(cond, lambda: make().start())
        self.open.append((cond, lambda: make().wait()))

    @staticmethod
    def when(cond, act):
        if cond is None:
            act()
        else:
            pl.when(cond)(act)

    def finish(self, since=0):
        for cond, act in self.open[since:]:
            self.when(cond, act)
        del self.open[since:]


def arrive(part, sem):
    pltpu.make_async_copy(view(part), view(part), view(sem)).wait()


def entry_barrier(geo, d, i, rho):
    sem = pltpu.get_barrier_semaphore()
    for k in range(1, V):
        pl.semaphore_signal(sem, inc=1, device_id=geo.dev(d, (i + k) % V, rho), device_id_type=MESH)
    for k in range(1, geo.q):
        pl.semaphore_signal(sem, inc=1, device_id=geo.dev((d + k) % geo.q, i, rho), device_id_type=MESH)
    pl.semaphore_wait(sem, V - 1 + geo.q - 1)


def cut_share(geo, i, buf, e_ref):
    q, base = geo.q, HEAD - 13 * i

    def put(j, e, row, n, start, stride):
        e_ref[j, e, pl.ds(row, n), :] = buf[pl.ds(start, n, stride=stride), :].astype(BF16)

    @pl.when(i < 2)
    def _():
        def body(n, c):
            e, s = n % q, n // q
            for b in range(8):
                put(b, e, mult(geo.qr * s, 16), geo.qr, base + 24 * geo.qr * e + 8 * s + b, 24)
            return c

        lax.fori_loop(0, 3 * q, body, 0)

    def rows_part(a0, ro, shift, count):
        def body(n, c):
            e, bl = n % q, n // q
            bb = bl + shift
            for b in range(8):
                put(
                    bb % V,
                    e,
                    mult(ro + geo.ap * (bb // V) + geo.ho * b, 16),
                    geo.ho,
                    base + a0 + 8 * (128 * bl + geo.ho * e) + b,
                    8,
                )
            return c

        lax.fori_loop(0, count * q, body, 0)

    def cols_part(a0, nr, ro):
        def body(n, c):
            e, t = n % q, n // q
            for b in range(8):
                put(b, e, mult(ro + nr * t, 16), nr, base + a0 + 32 * nr * e + 8 * t + b, 32)
            return c

        lax.fori_loop(0, 4 * q, body, 0)

    @pl.when(i == 2)
    def _():
        rows_part(0, 0, 0, 8)
        cols_part(8192, geo.u2, geo.ap)

    @pl.when((i == 3) | (i == 4))
    def _():
        cols_part(0, geo.u3, 0)

    @pl.when(i == 5)
    def _():
        cols_part(0, geo.u2, 0)
        rows_part(4096, geo.bp, 0, 8)

    @pl.when(i >= 6)
    def _():
        rows_part(0, 0, 4 * (i - 6), 12)


def owner_moves(geo, i, j):
    k = i - 6
    return (
        (i < 6, 0, mult(geo.seg * i, 16), geo.seg),
        (i >= 6, mult(geo.ap * k, 16), mult(6 * geo.seg + 2 * geo.ap * k, 16), geo.ap),
        ((i >= 6) & (j // 4 == k), mult(geo.ap * (1 - k), 16), 6 * geo.seg + geo.ap, geo.ap),
    )


def gather_kernel(geo, w_hbm, x_hbm, g_hbm, z_ref, x_ref, g_ref, v_ref, buf, hb, e_ref, vs, lsem, ssem, rsem):
    q, tl = geo.q, geo.tl
    d, i, rho = geo.place()
    z, c = i // 2, i % 2
    sib = 2 * z + 1 - c
    dev = partial(geo.dev, rho=rho)
    tx = Sends(ssem, rsem)
    send = tx.send

    load = pltpu.make_async_copy(w_hbm, buf.at[pl.ds(HEAD, OWN)], lsem.at[0])
    load.start()
    rows_own = pl.ds(mult(i * tl, 16), tl)
    own = [
        pltpu.make_async_copy(x_hbm, x_ref.at[rows_own], lsem.at[1]),
        pltpu.make_async_copy(g_hbm, g_ref.at[rows_own], lsem.at[2]),
    ]
    for cp in own:
        cp.start()
    entry_barrier(geo, d, i, rho)

    halo = pl.ds(OWN - 109, 109)
    send(i < V - 1, (w_hbm, halo), (hb, pl.ds(0, 109)), 0, dev(d, (i + 1) % V))

    def chain(a, src, ref):
        dst = (ref, rows_own)
        send(None, src, dst, 2 + a, dev(d, sib))
        send(z < CHIPS - 1, src, dst, 4 + 6 * a, dev(d, (i + 2) % V))
        send(z > 0, src, dst, 7 + 6 * a, dev(d, (i + V - 2) % V))

    def hop(a, ref, k):
        for s, sign in ((0, 1), (1, -1)):
            there = (z >= k + 1) if sign == 1 else (z + k + 1 < CHIPS)
            src_i = (i - 2 * sign * (k + 1) + 2 * V) % V
            rows = pl.ds(mult(src_i * tl, 16), tl)
            rs = 4 + 6 * a + 3 * s + k
            part = (ref, rows)

            @pl.when(there)
            def _():
                arrive(part, (rsem, rs))

            send(there, part, part, 2 + a, dev(d, sib))
            if k < CHIPS - 2:
                on = (z < CHIPS - 1) if sign == 1 else (z > 0)
                send(there & on, part, part, rs + 1, dev(d, (i + 2 * sign + V) % V))

    chain(0, x_hbm, x_ref)
    load.wait()

    @pl.when(i > 0)
    def _():
        arrive((hb, pl.ds(0, 109)), (rsem, 0))
        buf[pl.ds(HEAD - 104, 104), :] = hb[pl.ds(5, 104), :]

    @pl.when(i == V - 1)
    def _():
        vs[...] = buf[pl.ds(HEAD + OWN - VECS, VECS), :].astype(BF16)
        v_ref[...] = vs[...]

    cut_share(geo, i, buf, e_ref)
    hop(0, x_ref, 0)

    for k in range(1, V):
        send(i == V - 1, vs, v_ref, 1, dev(d, (i + k) % V))

    for k in range(1, CHIPS):
        for cc in range(2):
            j = (2 * (z + k) + cc) % V
            for ok, erow, zrow, n in owner_moves(geo, i, j):
                src = (e_ref, (j, d, pl.ds(erow, n)))
                send(ok, src, (z_ref, (d, pl.ds(zrow, n))), 16 + k, dev(d, j))
        if k < CHIPS - 1:
            hop(0, x_ref, k)
    whole = slice(None)
    for ok, erow, zrow, n in owner_moves(geo, i, sib):
        src = (e_ref, (sib, whole, pl.ds(erow, n)))
        send(ok, src, (z_ref, (whole, pl.ds(zrow, n))), 16, dev(d, sib))
    for ok, erow, zrow, n in owner_moves(geo, i, i):
        tx.copy(ok, (e_ref, (i, whole, pl.ds(erow, n))), (z_ref, (whole, pl.ds(zrow, n))))

    chain(1, g_hbm, g_ref)
    seg2 = 2 * geo.seg
    for k in range(1, CHIPS):
        rows = pl.ds(mult(((z + CHIPS - k) % CHIPS) * seg2, 16), seg2)
        arrive((z_ref, (0, pl.ds(0, seg2))), (rsem, 16 + k))
        for m in range(1, q):
            send(None, (z_ref, (d, rows)), (z_ref, (d, rows)), 20 + k, dev((d + m) % q, i))
        hop(1, g_ref, k - 1)
    for cp in own:
        cp.wait()

    @pl.when(i < V - 1)
    def _():
        arrive(v_ref, (rsem, 1))

    for ref, a in ((x_ref, 0), (g_ref, 1)):
        arrive((ref, pl.ds(0, CHIPS * tl)), (rsem, 2 + a))
    sib_owner_rows(geo, sib, z_ref, (rsem, 16))
    for k in range(1, CHIPS):
        arrive((z_ref, (pl.ds(0, q - 1), pl.ds(0, seg2))), (rsem, 20 + k))
    tx.finish()


def sib_owner_rows(geo, sib, z_ref, sem):
    _, i, _ = geo.place()

    @pl.when(sib < 6)
    def _():
        arrive((z_ref, (slice(None), pl.ds(0, geo.seg))), sem)

    @pl.when((sib >= 6) & (i // 4 == sib - 6))
    def _():
        arrive((z_ref, (slice(None), pl.ds(0, 2 * geo.ap))), sem)

    @pl.when((sib >= 6) & (i // 4 != sib - 6))
    def _():
        arrive((z_ref, (slice(None), pl.ds(0, geo.ap))), sem)


def gather(geo, w, x, g):
    q = geo.q
    vm = pl.BlockSpec(memory_space=pltpu.VMEM)
    hbm = pl.BlockSpec(memory_space=pl.ANY)
    return pl.pallas_call(
        partial(gather_kernel, geo),
        out_shape=(
            jax.ShapeDtypeStruct((q, geo.zr, 128), BF16),
            jax.ShapeDtypeStruct((geo.t, D), BF16),
            jax.ShapeDtypeStruct((geo.t, D), BF16),
            jax.ShapeDtypeStruct((VECS, 128), BF16),
        ),
        in_specs=[hbm] * 3,
        out_specs=(vm,) * 4,
        scratch_shapes=[
            pltpu.VMEM((HEAD + OWN + 3, 128), F32),
            pltpu.VMEM((112, 128), F32),
            pltpu.VMEM((V, q, geo.er, 128), BF16),
            pltpu.VMEM((VECS, 128), BF16),
            pltpu.SemaphoreType.DMA((4,)),
            pltpu.SemaphoreType.DMA((80,)),
            pltpu.SemaphoreType.DMA((24,)),
        ],
        compiler_params=pltpu.CompilerParams(
            collective_id=0, has_side_effects=True, vmem_limit_bytes=60 << 20
        ),
        name="gather",
    )(w, x, g)


def rot_tables(t):
    half = ROT // 2
    freq = (10000.0 ** (-2.0 * np.arange(half, dtype=np.float32) / ROT)).astype(np.float32)
    ang = np.arange(t, dtype=np.float32)[:, None] * freq[None, :]
    cos = np.ones((t, 128), np.float32)
    sin = np.zeros((t, 128), np.float32)
    for h in range(2):
        for k in range(2):
            lo = 64 * h + half * k
            cos[:, lo : lo + half] = np.cos(ang)
            sin[:, lo : lo + half] = np.sin(ang) * (1 if k else -1)
    return jnp.asarray(cos), jnp.asarray(sin)


def rot(v, cos, sin, lane, back):
    up = pltpu.roll(v, 120, 1)
    down = pltpu.roll(v, 8, 1)
    partner = jnp.where(lane % 16 < 8, up, down)
    turn = partner * sin
    return v * cos - turn if back else v * cos + turn


def compute_kernel(
    geo, z_ref, x_ref, g_ref, v_ref, cos_ref, sin_ref, po_ref, pa_ref, gz_ref, vp_ref,
    vf, rowv, wq, wo, wu, wd, xh, n1, n2, qs, ks, vv, hid, gp, du, ob, do, dqkv, dqs, dk, dv, acc,
):
    t = geo.t
    d, j, rho = geo.place()
    mats = (wq, wo, wu, wd)
    nrb = t // RB
    for e, zrow, n, m, row, lane in geo.maps():
        mats[m][row : row + n, lane : lane + 128] = z_ref[e, zrow : zrow + n, :]
    vf[...] = v_ref[...].astype(F32)
    for k in range(9):
        for b in range(8):
            rowv[k : k + 1, 128 * b : 128 * b + 128] = vf[8 * k + b : 8 * k + b + 1, :]
    acc[...] = jnp.zeros_like(acc)
    dk[...] = jnp.zeros_like(dk)
    dv[...] = jnp.zeros_like(dv)

    def rb_of(r):
        return pl.ds(mult(r * RB, RB), RB)

    lane = lax.broadcasted_iota(jnp.int32, (RB, 128), 1)

    def forward(r, carry):
        rb = rb_of(r)
        x = x_ref[rb, :].astype(F32)
        mean = jnp.mean(x, axis=1, keepdims=True)
        mid = x - mean
        var = jnp.mean(mid * mid, axis=1, keepdims=True)
        inv = lax.rsqrt(var + 1e-05)
        xhat = mid * inv
        xh[rb, 0:1] = mean
        xh[rb, 1:2] = inv
        one = (xhat * rowv[0:1, :] + rowv[1:2, :]).astype(BF16)
        two = (xhat * rowv[2:3, :] + rowv[3:4, :]).astype(BF16)
        n1[rb, :] = one
        n2[rb, :] = two
        qkv = dot(one, wq[...])
        cos, sin = cos_ref[rb, :], sin_ref[rb, :]
        qh = qkv[:, 0:128] + vf[pl.ds(32 + j, 1), :]
        kh = qkv[:, 128:256] + vf[pl.ds(40 + j, 1), :]
        vh = qkv[:, 256:384] + vf[pl.ds(48 + j, 1), :]
        qs[rb, :] = (rot(qh, cos, sin, lane, False) * 0.125).astype(BF16)
        ks[rb, :] = rot(kh, cos, sin, lane, False).astype(BF16)
        vv[rb, :] = vh.astype(BF16)
        up = dot(two, wu[...])
        for b in range(4):
            cols = slice(128 * b, 128 * b + 128)
            u = up[:, cols] + vf[pl.ds(72 + 8 * b + j, 1), :]
            phi = 0.5 + 0.5 * lax.erf(u * (1.0 / math.sqrt(2.0)))
            hid[rb, cols] = (u * phi).astype(BF16)
            gp[rb, cols] = phi + u * (jnp.exp(-0.5 * u * u) * (1.0 / math.sqrt(2.0 * math.pi)))
        return carry

    lax.fori_loop(0, nrb, forward, 0)

    def back_mlp(r, carry):
        rb = rb_of(r)
        g = g_ref[rb, :]
        dh = dot_nt(g, wd[...])
        low = (dh * gp[rb, :]).astype(BF16)
        du[rb, :] = low
        do[rb, :] = dot_nt(g, wo[...]).astype(BF16)
        acc[4:5, :] += jnp.sum(g.astype(F32), axis=0, keepdims=True)
        acc[5:6, 0:512] += jnp.sum(low.astype(F32), axis=0, keepdims=True)
        return carry

    lax.fori_loop(0, nrb, back_mlp, 0)

    left = lax.broadcasted_iota(jnp.int32, (RB, 128), 1) < 64
    diag = lax.broadcasted_iota(jnp.int32, (RB, RB), 0) >= lax.broadcasted_iota(jnp.int32, (RB, RB), 1)
    zero = jnp.zeros((), BF16)
    for r in range(nrb):
        rb = slice(r * RB, r * RB + RB)
        n = (r + 1) * RB
        outs, dqh = [], []
        for h in range(2):
            mine = left if h == 0 else jnp.logical_not(left)
            qm = jnp.where(mine, qs[rb, :], zero)
            gm = jnp.where(mine, do[rb, :], zero)
            s = dot_nt(qm, ks[0:n, :])
            tail = jnp.where(diag, s[:, n - RB : n], -1e30)
            s = tail if r == 0 else jnp.concatenate([s[:, : n - RB], tail], axis=1)
            top = jnp.max(s, axis=1, keepdims=True)
            ex = jnp.exp(s - top)
            prob = ex * (1.0 / jnp.sum(ex, axis=1, keepdims=True))
            low = prob.astype(BF16)
            outs.append(dot(low, vv[0:n, :]))
            dp = dot_nt(gm, vv[0:n, :])
            delta = jnp.sum(prob * dp, axis=1, keepdims=True)
            ds = (prob * (dp - delta)).astype(BF16)
            dqh.append(dot(ds, ks[0:n, :]))
            dk[0:n, :] += dot_tn(ds, qm)
            dv[0:n, :] += dot_tn(low, gm)
        ob[rb, :] = jnp.where(left, outs[0], outs[1]).astype(BF16)
        dqs[rb, :] = jnp.where(left, dqh[0], dqh[1])

    def back(r, carry):
        rb = rb_of(r)
        cos, sin = cos_ref[rb, :], sin_ref[rb, :]
        po_ref[rb, :] = (dot(hid[rb, :], wd[...]) + dot(ob[rb, :], wo[...])).astype(BF16)
        low = jnp.concatenate(
            [
                (rot(dqs[rb, :], cos, sin, lane, True) * 0.125).astype(BF16),
                rot(dk[rb, :], cos, sin, lane, True).astype(BF16),
                dv[rb, :].astype(BF16),
            ],
            axis=1,
        )
        dqkv[rb, :] = low
        acc[6:7, 0:384] += jnp.sum(low.astype(F32), axis=0, keepdims=True)
        xhat = (x_ref[rb, :].astype(F32) - xh[rb, 0:1]) * xh[rb, 1:2]
        d1 = dot_nt(low, wq[...])
        acc[0:1, :] += jnp.sum(d1 * xhat, axis=0, keepdims=True)
        acc[1:2, :] += jnp.sum(d1, axis=0, keepdims=True)
        d2 = dot_nt(du[rb, :], wu[...])
        acc[2:3, :] += jnp.sum(d2 * xhat, axis=0, keepdims=True)
        acc[3:4, :] += jnp.sum(d2, axis=0, keepdims=True)
        pa_ref[rb, :] = (d1 * rowv[0:1, :] + d2 * rowv[2:3, :]).astype(BF16)
        return carry

    lax.fori_loop(0, nrb, back, 0)
    def grad_cols(left_ref, right_ref, out, blocks):
        def body(k, carry):
            cols = pl.ds(mult(k * 256, 256), 256)
            out[cols, :] = dot_tn(left_ref[:, cols], right_ref[...]).astype(BF16)
            return carry

        lax.fori_loop(0, blocks, body, 0)

    grad_cols(hid, g_ref, wd, 2)
    grad_cols(n2, du, wu, 4)
    grad_cols(n1, dqkv, wq, 4)
    wo[...] = dot_tn(ob[...], g_ref[...]).astype(BF16)
    for e, zrow, n, m, row, lane in geo.maps():
        gz_ref[e, zrow : zrow + n, :] = mats[m][row : row + n, lane : lane + 128]
    vp_ref[...] = jnp.zeros_like(vp_ref)
    first = jnp.where(j == 0, 1.0, 0.0)
    for b in range(8):
        cols = slice(128 * b, 128 * b + 128)
        for k in range(4):
            vp_ref[8 * k + b : 8 * k + b + 1, :] = acc[k : k + 1, cols]
        for k in (7, 8):
            vp_ref[8 * k + b : 8 * k + b + 1, :] = acc[4:5, cols] * first
    for k in range(3):
        vp_ref[pl.ds(32 + 8 * k + j, 1), :] = acc[6:7, 128 * k : 128 * k + 128]
    for k in range(4):
        vp_ref[pl.ds(72 + 8 * k + j, 1), :] = acc[5:6, 128 * k : 128 * k + 128]


def compute(geo, zs, x, g, v):
    q, t = geo.q, geo.t
    vm = pl.BlockSpec(memory_space=pltpu.VMEM)
    cos, sin = rot_tables(t)
    return pl.pallas_call(
        partial(compute_kernel, geo),
        out_shape=(
            jax.ShapeDtypeStruct((t, D), BF16),
            jax.ShapeDtypeStruct((t, D), BF16),
            jax.ShapeDtypeStruct((q, geo.zr, 128), BF16),
            jax.ShapeDtypeStruct((VECS, 128), F32),
        ),
        in_specs=[vm] * 6,
        out_specs=(vm,) * 4,
        scratch_shapes=[
            pltpu.VMEM((VECS, 128), F32),
            pltpu.VMEM((16, D), F32),
            pltpu.VMEM((D, 384), BF16),
            pltpu.VMEM((128, D), BF16),
            pltpu.VMEM((D, 512), BF16),
            pltpu.VMEM((512, D), BF16),
            pltpu.VMEM((t, 2), F32),
            pltpu.VMEM((t, D), BF16),
            pltpu.VMEM((t, D), BF16),
            pltpu.VMEM((t, 128), BF16),
            pltpu.VMEM((t, 128), BF16),
            pltpu.VMEM((t, 128), BF16),
            pltpu.VMEM((t, 512), BF16),
            pltpu.VMEM((t, 512), F32),
            pltpu.VMEM((t, 512), BF16),
            pltpu.VMEM((t, 128), BF16),
            pltpu.VMEM((t, 128), BF16),
            pltpu.VMEM((t, 384), BF16),
            pltpu.VMEM((t, 128), F32),
            pltpu.VMEM((t, 128), F32),
            pltpu.VMEM((t, 128), F32),
            pltpu.VMEM((8, D), F32),
        ],
        compiler_params=pltpu.CompilerParams(vmem_limit_bytes=63 << 20),
        name="compute",
    )(zs, x, g, v, cos, sin)


def scatter_kernel(
    geo, gz_ref, po_ref, pa_ref, vp_ref, v_ref, x_ref, g_ref, w_hbm, m_hbm, s_hbm,
    lo_ref, tg_ref, wg_hbm, nw_hbm, nm_hbm, ns_hbm,
    wb, mb, sb, ob, gb, hb, rz, rb, fb, sibo, siba, rcvo, rcva, vr, vsum, vq, lsem, ssem, rsem,
):
    q, tl = geo.q, geo.tl
    d, i, rho = geo.place()
    z, c = i // 2, i % 2
    sib = 2 * z + 1 - c
    dev = partial(geo.dev, rho=rho)
    tx = Sends(ssem, rsem)
    send = tx.send
    whole = slice(None)
    loads = [
        pltpu.make_async_copy(h, b.at[pl.ds(0, OWN)], lsem.at[k])
        for k, (h, b) in enumerate(((w_hbm, wb), (m_hbm, mb), (s_hbm, sb)))
    ]
    entry_barrier(geo, d, i, rho)
    for k in range(1, q):
        e = (d + k) % q
        send(None, (gz_ref, e), (rb, k - 1), 7 + k, dev(e, i))
    for a, (p, sb_) in enumerate(((po_ref, sibo), (pa_ref, siba))):
        for k in range(CHIPS):
            rows = pl.ds(mult((2 * k + 1 - c) * tl, 16), tl)
            send(None, (p, rows), (sb_, k), a, dev(d, sib))
    send(i < V - 1, vp_ref, (vr, i), 4, dev(d, V - 1))
    for ld in loads:
        ld.start()
    for a, (p, sn, rc) in enumerate(((po_ref, sibo, rcvo), (pa_ref, siba, rcva))):
        arrive(sn, (rsem, a))
        for k in range(CHIPS):
            rows = pl.ds(mult((2 * k + c) * tl, 16), tl)
            sn[k] = (p[rows, :].astype(F32) + sn[k].astype(F32)).astype(BF16)
        for k in range(1, CHIPS):
            to = (z + k) % CHIPS
            send(None, (sn, to), (rc, k - 1), 2 + a, dev(d, 2 * to + c))
    for k in range(1, q):
        arrive((rb, k - 1), (rsem, 7 + k))

    step = 256

    def add(n, carry):
        rows = pl.ds(mult(n * step, step), step)
        tot = gz_ref[d, rows, :].astype(F32)
        for k in range(q - 1):
            tot = tot + rb[k, rows, :].astype(F32)
        rz[rows, :] = tot.astype(BF16)
        return carry

    lax.fori_loop(0, geo.zr // step, add, 0)
    for k in range(V):
        o = (i + k) % V
        at = len(tx.open)
        for m, (ok, erow, zrow, n) in enumerate(owner_moves(geo, o, i)):
            src, dst = (rz, pl.ds(zrow, n)), (fb, (i, d, pl.ds(erow, n)))
            if k:
                send(ok, src, dst, 17 if m == 2 else 16, dev(d, o))
            else:
                tx.copy(ok, src, dst)
        if k == 0:
            tx.finish(at)
    @pl.when(i < 6)
    def _():
        arrive((fb, (pl.ds(0, V - 1), 0, pl.ds(0, geo.seg))), (rsem, 16))

    @pl.when(i == 6)
    def _():
        arrive((fb, (pl.ds(0, V - 1), 0, pl.ds(0, geo.ap))), (rsem, 16))
        arrive((fb, (pl.ds(0, 4), 0, pl.ds(0, geo.ap))), (rsem, 17))

    @pl.when(i == 7)
    def _():
        arrive((fb, (pl.ds(0, V - 1), 0, pl.ds(0, geo.ap))), (rsem, 16))
        arrive((fb, (pl.ds(0, 3), 0, pl.ds(0, geo.ap))), (rsem, 17))

    for k in range(1, q):
        e = (d + k) % q
        small, large = (fb, (whole, d, pl.ds(0, geo.seg))), (fb, (whole, d))
        send(i < 6, small, small, 19 + k, dev(e, i))
        send(i >= 6, large, large, 19 + k, dev(e, i))

    arrive(rcvo, (rsem, 2))
    arrive(rcva, (rsem, 3))
    vecf = lambda k: jnp.concatenate(
        [v_ref[8 * k + b : 8 * k + b + 1, :].astype(F32) for b in range(8)], axis=1
    )
    bias = vecf(7) + vecf(8)
    x = x_ref[...].astype(F32)
    so = sibo[z].astype(F32) + rcvo[0].astype(F32) + rcvo[1].astype(F32) + rcvo[2].astype(F32)
    lo_ref[...] = (x + so + bias).astype(BF16)
    sa = siba[z].astype(F32) + rcva[0].astype(F32) + rcva[1].astype(F32) + rcva[2].astype(F32)
    mid = x - jnp.mean(x, axis=1, keepdims=True)
    inv = lax.rsqrt(jnp.mean(mid * mid, axis=1, keepdims=True) + 1e-05)
    xhat = mid * inv
    dx = inv * (sa - jnp.mean(sa, axis=1, keepdims=True) - xhat * jnp.mean(sa * xhat, axis=1, keepdims=True))
    tg_ref[...] = g_ref[...].astype(F32) + dx

    @pl.when(i == V - 1)
    def _():
        arrive((vr, pl.ds(0, V - 1)), (rsem, 4))
        tot = vp_ref[...]
        for k in range(V - 1):
            tot = tot + vr[k]
        vsum[...] = tot

    for k in range(1, q):
        send(i == V - 1, vsum, (vq, k - 1), 5, dev((d + k) % q, i))

    for k in range(1, q):
        @pl.when(i < 6)
        def _():
            arrive((fb, (whole, 0, pl.ds(0, geo.seg))), (rsem, 19 + k))

        @pl.when(i >= 6)
        def _():
            arrive((fb, (whole, 0)), (rsem, 19 + k))

    paste_share(geo, i, gb, fb)

    @pl.when(i > 0)
    def _():
        hb[1] = gb[pl.ds(0, VECS), :]

    send(i > 0, (hb, 1), (hb, 0), 6, dev(d, (i + V - 1) % V))

    @pl.when(i < V - 1)
    def _():
        arrive((hb, 0), (rsem, 6))
        gb[pl.ds(ALI, VECS), :] = hb[0]

    @pl.when(i == V - 1)
    def _():
        arrive(vq, (rsem, 5))
        tot = vsum[...]
        for k in range(q - 1):
            tot = tot + vq[k]
        gb[pl.ds(ALI, VECS), :] = tot

    for ld in loads:
        ld.wait()
    rows_n = 1024
    full = OWN // rows_n
    stores = []

    def adam(n, carry):
        rows = pl.ds(mult(n * rows_n, rows_n), rows_n)
        adam_rows(i, rows, n * rows_n, rows_n, wb, mb, sb, ob, gb)
        for k, (h, b) in enumerate(((wg_hbm, ob), (nw_hbm, wb), (nm_hbm, mb), (ns_hbm, sb))):
            pltpu.make_async_copy(b.at[rows], h.at[rows], lsem.at[4 + k]).start()
        return carry

    lax.fori_loop(0, full, adam, 0)
    rest = OWN - full * rows_n
    adam_rows(i, pl.ds(full * rows_n, 16), full * rows_n, 16, wb, mb, sb, ob, gb)
    for k, (h, b) in enumerate(((wg_hbm, ob), (nw_hbm, wb), (nm_hbm, mb), (ns_hbm, sb))):
        rows = pl.ds(full * rows_n, rest)
        pltpu.make_async_copy(b.at[rows], h.at[rows], lsem.at[4 + k]).start()
    for k, (h, b) in enumerate(((wg_hbm, ob), (nw_hbm, wb), (nm_hbm, mb), (ns_hbm, sb))):
        pltpu.make_async_copy(b.at[pl.ds(0, OWN)], h, lsem.at[4 + k]).wait()
    tx.finish()


def adam_rows(i, rows, start, n, wb, mb, sb, ob, gb):
    g = gb[pl.ds(13 * i + start, n), :]
    w = wb[rows, :]
    m = BETA_ONE * mb[rows, :] + (1.0 - BETA_ONE) * g
    s = BETA_TWO * sb[rows, :] + (1.0 - BETA_TWO) * g * g
    ob[rows, :] = g
    mb[rows, :] = m
    sb[rows, :] = s
    mh = m * (1.0 / (1.0 - BETA_ONE**STEP))
    vh = s * (1.0 / (1.0 - BETA_TWO**STEP))
    wb[rows, :] = w - LEARN_RATE * (mh / (jnp.sqrt(vh) + EPSILON) + DECAY_RATE * w)


def paste_share(geo, i, gb, f_ref):
    q = geo.q

    def put(j, e, row, n, start, stride):
        gb[pl.ds(start, n, stride=stride), :] = f_ref[j, e, pl.ds(row, n), :].astype(F32)

    @pl.when(i < 2)
    def _():
        def body(n, c):
            e, s = n % q, n // q
            for b in range(8):
                put(b, e, mult(geo.qr * s, 16), geo.qr, 24 * geo.qr * e + 8 * s + b, 24)
            return c

        lax.fori_loop(0, 3 * q, body, 0)

    def rows_part(a0, ro, shift, count):
        def body(n, c):
            e, bl = n % q, n // q
            bb = bl + shift
            for b in range(8):
                put(
                    bb % V,
                    e,
                    mult(ro + geo.ap * (bb // V) + geo.ho * b, 16),
                    geo.ho,
                    a0 + 8 * (128 * bl + geo.ho * e) + b,
                    8,
                )
            return c

        lax.fori_loop(0, count * q, body, 0)

    def cols_part(a0, nr, ro):
        def body(n, c):
            e, t = n % q, n // q
            for b in range(8):
                put(b, e, mult(ro + nr * t, 16), nr, a0 + 32 * nr * e + 8 * t + b, 32)
            return c

        lax.fori_loop(0, 4 * q, body, 0)

    @pl.when(i == 2)
    def _():
        rows_part(0, 0, 0, 8)
        cols_part(8192, geo.u2, geo.ap)

    @pl.when((i == 3) | (i == 4))
    def _():
        cols_part(0, geo.u3, 0)

    @pl.when(i == 5)
    def _():
        cols_part(0, geo.u2, 0)
        rows_part(4096, geo.bp, 0, 8)

    @pl.when(i >= 6)
    def _():
        rows_part(0, 0, 4 * (i - 6), 12)


def scatter(geo, gz, po, pa, vp, v, x, g, w, m, s):
    q, tl = geo.q, geo.tl
    vm = pl.BlockSpec(memory_space=pltpu.VMEM)
    hbm = pl.BlockSpec(memory_space=pl.ANY)
    flat = jax.ShapeDtypeStruct((OWN, 128), F32)
    big = pltpu.VMEM((OWN + 3, 128), F32)
    line = pltpu.VMEM((CHIPS, tl, D), BF16)
    line3 = pltpu.VMEM((CHIPS - 1, tl, D), BF16)
    return pl.pallas_call(
        partial(scatter_kernel, geo),
        out_shape=(
            jax.ShapeDtypeStruct((tl, D), BF16),
            jax.ShapeDtypeStruct((tl, D), F32),
            flat, flat, flat, flat,
        ),
        in_specs=[vm] * 7 + [hbm] * 3,
        out_specs=(vm, vm, hbm, hbm, hbm, hbm),
        scratch_shapes=[
            big, big, big, big,
            pltpu.VMEM((ALI + 128, 128), F32),
            pltpu.VMEM((2, VECS, 128), F32),
            pltpu.VMEM((geo.zr, 128), BF16),
            pltpu.VMEM((q - 1, geo.zr, 128), BF16),
            pltpu.VMEM((V, q, geo.er, 128), BF16),
            line, line, line3, line3,
            pltpu.VMEM((V - 1, VECS, 128), F32),
            pltpu.VMEM((VECS, 128), F32),
            pltpu.VMEM((q - 1, VECS, 128), F32),
            pltpu.SemaphoreType.DMA((8,)),
            pltpu.SemaphoreType.DMA((80,)),
            pltpu.SemaphoreType.DMA((32,)),
        ],
        compiler_params=pltpu.CompilerParams(
            collective_id=1, has_side_effects=True, vmem_limit_bytes=63 << 20
        ),
        name="scatter",
    )(gz, po, pa, vp, v, x, g, w, m, s)


def local(mesh, tokens, cotangent, weights, first_moment, second_moment):
    rep = mesh.shape["ctx"] // V
    rows = tokens.shape[1]
    x, g = tokens[0], cotangent[0]
    flats = [weights, first_moment, second_moment]
    if rep > 1:
        groups = [[rep * k + r for r in range(rep)] for k in range(V)]
        join = lambda a: lax.all_gather(a, "ctx", axis=0, axis_index_groups=groups, tiled=True)
        x, g = join(x), join(g)
        flats = [join(a) for a in flats]
    w, m, s = [a.reshape(OWN, 128) for a in flats]
    geo = Geo(mesh, x.shape[0] * V)
    zs, xs, gs, v = gather(geo, w, x, g)
    po, pa, gz, vp = compute(geo, zs, xs, gs, v)
    outs = list(scatter(geo, gz, po, pa, vp, v, x, g, w, m, s))
    outs[2:] = [a.reshape(-1) for a in outs[2:]]
    if rep > 1:
        r = lax.axis_index("ctx") % rep
        outs = [lax.dynamic_slice_in_dim(a, r * (a.shape[0] // rep), a.shape[0] // rep, 0) for a in outs]
    return (outs[0][None], outs[1][None], *outs[2:])


def solution(mesh):
    return jax.shard_map(
        partial(local, mesh),
        mesh=mesh,
        in_specs=(P("dp", "ctx", None), P("dp", "ctx", None), P("ctx"), P("ctx"), P("ctx")),
        out_specs=(P("dp", "ctx", None), P("dp", "ctx", None), P("ctx"), P("ctx"), P("ctx"), P("ctx")),
        check_vma=False,
    )
```

time: 1960 us -> 262 us (0.13)
  the two profiles are of different devices: /device:TPU:15 before, /device:TPU:17 now
where the time goes in v1:
time: 262 us
  Pallas kernels  239 us (91%)
  local copies, waits for them, and re-layouts  21.6 us (8%)
    pallas_call x1, Pallas kernels, scatter(): pl.pallas_call(partial(scatter_kernel, geo), out_shape=(jax.ShapeDtypeStr...  137 us
    pallas_call x1, Pallas kernels, gather(): pl.pallas_call(partial(gather_kernel, geo), out_shape=(jax.ShapeDtypeStru...  69.4 us
    pallas_call x1, Pallas kernels, compute(): pl.pallas_call(partial(compute_kernel, geo), out_shape=(jax.ShapeDtypeStr...  32.7 us
    unnamed x16, local copies, waits for them, and re-layouts  21.6 us

profile of v1, /device:TPU:17, one launch (start us, length us, event | category | flops | bytes accessed | tf_op | source)
XLA Modules:
  0.0 261.7 jit_solution(792707241418867943)
XLA Ops:
  0.6 69.4 %gather.1 = (bf16[4,3072,128]{2,1,0:T(8,128)(2,1)}, bf16[1024,1024]{1,0:T(8,128)(2,1)}, bf16[1024,1024]{1,0:T(8,128)(2,1)}, bf16[104,128]{1,0:T(8,128)(2,1)}) custom-call(f32[12301,128]{1,0:T(8,128)} %bitcast.11, bf16[128,1024]{1,0:T(8,128)(2,1)} %bitcast.23, bf16[128,1024]{1,0:T(8,128)(2,1)} %bitcast.25), custom_call_target="tpu_custom_call" | custom-call | tf_op jit(solution)/shard_map/gather/pallas_call | solution.py:355
  70.0 32.7 %compute.1 = (bf16[1024,1024]{1,0:T(8,128)(2,1)}, bf16[1024,1024]{1,0:T(8,128)(2,1)}, bf16[4,3072,128]{2,1,0:T(8,128)(2,1)}, f32[104,128]{1,0:T(8,128)}) custom-call(bf16[4,3072,128]{2,1,0:T(8,128)(2,1)} %get-tuple-element.20.z_ref, bf16[1024,1024]{1,0:T(8,128)(2,1)} %get-tuple-element.21.x_ref, bf16[1024,1024]{1,0:T(8,128)(2,1)} %get-tuple-element.22.g_ref, ...), custom_call_target="tpu_custom_call" | custom-call | tf_op jit(solution)/shard_map/compute/pallas_call | solution.py:557
  102.7 137.3 %scatter.1 = (bf16[128,1024]{1,0:T(8,128)(2,1)}, f32[128,1024]{1,0:T(8,128)}, f32[12301,128]{1,0:T(8,128)}, f32[12301,128]{1,0:T(8,128)}, f32[12301,128]{1,0:T(8,128)}, /*index=5*/f32[12301,128]{1,0:T(8,128)}) custom-call(bf16[4,3072,128]{2,1,0:T(8,128)(2,1)} %get-tuple-element.24.gz_ref, bf16[1024,1024]{1,0:T(8,128)(2,1)} %get-tuple-element.25.po_ref, ...), custom_call_target="tpu_custom_call" | custom-call | tf_op jit(solution)/shard_map/scatter/pallas_call | solution.py:840
  240.1 1.7 copy.19
  241.8 1.9 copy.20
  243.6 0.0 copy-start
  243.6 0.0 slice-start.2
  243.6 5.4 %copy.21 = f32[1574528]{0:T(1024)} copy(f32[1574528]{0:T(1024)} %bitcast.20) | data formatting | bytes 12596224
  249.1 1.5 copy-done
  250.6 0.0 slice-start.3
  250.6 0.0 slice-start
  250.6 3.4 %copy.22 = f32[1574528]{0:T(1024)} copy(f32[1574528]{0:T(1024)S(1)} %bitcast.19) | data formatting | bytes 12596224
  254.0 0.0 slice-done.2
  254.0 0.2 slice-done.3
  254.1 0.0 slice-start.1
  254.1 3.4 %copy.23 = f32[1574528]{0:T(1024)} copy(f32[1574528]{0:T(1024)S(1)} %bitcast.18) | data formatting | bytes 12596224
  257.5 0.0 slice-done
  257.5 1.2 slice-done.1
  258.8 2.9 %copy.24 = f32[1574528]{0:T(1024)} copy(f32[1574528]{0:T(1024)S(1)} %bitcast.15) | data formatting | bytes 12596224
  (2 shorter events, 0.0 us)
Async XLA Ops:
  243.6 6.9 %copy-start = (f32[12301,128]{1,0:T(8,128)S(1)}, f32[12301,128]{1,0:T(8,128)}, u32[]{:S(2)}) copy-start(f32[12301,128]{1,0:T(8,128)} %get-tuple-element.31) | copy-start | bytes 18894340
  243.6 10.3 %slice-start.2 = ((s8[6299648]{0:T(1024)(128)(4,1)}), s8[4194304]{0:T(1024)(128)(4,1)S(1)}, s32[]{:S(2)}) async-start(s8[6299648]{0:T(1024)(128)(4,1)} %bitcast.16), calls=%async_computation.2 | async-start | bytes 8388608
  250.6 3.6 %slice-start.3 = ((s8[6299648]{0:T(1024)(128)(4,1)}), s8[2105344]{0:T(1024)(128)(4,1)S(1)}, s32[]{:S(2)}) async-start(s8[6299648]{0:T(1024)(128)(4,1)} %bitcast.16), calls=%async_computation.3 | async-start | bytes 4210688
  250.6 7.0 %slice-start = ((s8[6299648]{0:T(1024)(128)(4,1)}), s8[4194304]{0:T(1024)(128)(4,1)S(1)}, s32[]{:S(2)}) async-start(s8[6299648]{0:T(1024)(128)(4,1)} %bitcast.13), calls=%async_computation | async-start | bytes 8388608
  254.1 4.6 %slice-start.1 = ((s8[6299648]{0:T(1024)(128)(4,1)}), s8[2105344]{0:T(1024)(128)(4,1)S(1)}, s32[]{:S(2)}) async-start(s8[6299648]{0:T(1024)(128)(4,1)} %bitcast.13), calls=%async_computation.1 | async-start | bytes 4210688

commit v2 on v1

v2 whole, which is shorter than its diff:
```python
from functools import partial
import math

import numpy as np
import jax
import jax.numpy as jnp
from jax import lax
from jax.experimental import pallas as pl
from jax.experimental.pallas import tpu as pltpu
from jax.sharding import PartitionSpec as P

D = 1024
FF = 4096
HEADS = 16
HEAD_DIM = 64
ROT = 16
STEP = 3
BETA_ONE = 0.9
BETA_TWO = 0.95
LEARN_RATE = 0.004
DECAY_RATE = 0.1
EPSILON = 1e-08

F32 = jnp.float32
BF16 = jnp.bfloat16
MESH = pl.DeviceIdType.MESH
V = 8
CHIPS = V // 2
OWN = 12301
ALI = 12288
VECS = 104
HEAD = 112
RB = 256
SPREAD = 31
SUMS = 80


class Geo:
    def __init__(self, mesh, tokens):
        self.q = mesh.shape["dp"]
        self.rep = mesh.shape["ctx"] // V
        self.tl = tokens // V
        self.t = tokens
        q = self.q
        self.qr = 512 // q
        self.ho = 128 // q
        self.u2 = 128 // q
        self.u3 = 384 // q
        self.seg = 1536 // q
        self.zr = V * self.seg
        self.ap = 1024 // q
        self.bp = 512 // q
        self.er = 2 * self.ap
        self.tight = tokens > 1024
        self.rba = RB // 2 if self.tight else RB
        self.square = q == 4
        self.ss = max(4, q - 1)

    def place(self):
        d = lax.axis_index("dp")
        a = lax.axis_index("ctx")
        return d, a // self.rep, a % self.rep

    def dev(self, e, j, rho):
        return {"dp": e, "ctx": j * self.rep + rho}

    def maps(self):
        q, out = self.q, []
        for e in range(q):
            for i in range(2):
                for s in range(3):
                    out.append((e, self.seg * i + self.qr * s, self.qr, 0, 512 * i + self.qr * e, 128 * s))
            for b in range(8):
                out.append((e, 2 * self.seg + self.ho * b, self.ho, 1, self.ho * e, 128 * b))
            parts = (
                (0, self.u2, 2 * self.seg + self.ap),
                (128, self.u3, 3 * self.seg),
                (512, self.u3, 4 * self.seg),
                (896, self.u2, 5 * self.seg),
            )
            for r0, nr, off in parts:
                for t in range(4):
                    out.append((e, off + nr * t, nr, 2, r0 + nr * e, 128 * t))
            for t in range(4):
                for b in range(8):
                    row = 5 * self.seg + self.bp + self.ap * t + self.ho * b
                    out.append((e, row, self.ho, 3, 128 * t + self.ho * e, 128 * b))
        return out


def dot(a, b):
    return jnp.dot(a, b, preferred_element_type=F32)


def dot_nt(a, b):
    return lax.dot_general(a, b, (((1,), (1,)), ((), ())), preferred_element_type=F32)


def dot_tn(a, b):
    return lax.dot_general(a, b, (((0,), (0,)), ((), ())), preferred_element_type=F32)


def mult(x, n):
    return pl.multiple_of(x, n)


def view(part):
    return part[0].at[part[1]] if isinstance(part, tuple) else part


def rcopy(src, dst, ssem, rsem, dev):
    return pltpu.make_async_remote_copy(
        src_ref=view(src),
        dst_ref=view(dst),
        send_sem=view(ssem),
        recv_sem=view(rsem),
        device_id=dev,
        device_id_type=MESH,
    )


class Sends:
    def __init__(self, ssem, rsem, used=None):
        self.ssem, self.rsem, self.used, self.open = ssem, rsem, used or [0], []

    def group(self):
        return Sends(self.ssem, self.rsem, self.used)

    def slot(self):
        self.used[0] += 1
        return (self.ssem, self.used[0] - 1)

    def send(self, cond, src, dst, rs, dev):
        slot = self.slot()
        make = lambda: rcopy(src, dst, slot, (self.rsem, rs), dev)
        self.when(cond, lambda: make().start())
        self.open.append((cond, lambda: make().wait_send()))

    def copy(self, cond, src, dst):
        slot = self.slot()
        make = lambda: pltpu.make_async_copy(view(src), view(dst), view(slot))
        self.when(cond, lambda: make().start())
        self.open.append((cond, lambda: make().wait()))

    @staticmethod
    def when(cond, act):
        if cond is None:
            act()
        else:
            pl.when(cond)(act)

    def finish(self):
        for cond, act in self.open:
            self.when(cond, act)
        self.open.clear()


def arrive(part, sem):
    pltpu.make_async_copy(view(part), view(part), view(sem)).wait()


def entry_barrier(geo, d, i, rho):
    sem = pltpu.get_barrier_semaphore()
    for k in range(1, V):
        pl.semaphore_signal(sem, inc=1, device_id=geo.dev(d, (i + k) % V, rho), device_id_type=MESH)
    for k in range(1, geo.q):
        pl.semaphore_signal(sem, inc=1, device_id=geo.dev((d + k) % geo.q, i, rho), device_id_type=MESH)
    pl.semaphore_wait(sem, V - 1 + geo.q - 1)


def cut_share(geo, i, buf, e_ref):
    q, base = geo.q, HEAD - 13 * i

    def put(j, e, row, n, start, stride):
        e_ref[j, e, pl.ds(row, n), :] = buf[pl.ds(start, n, stride=stride), :].astype(BF16)

    @pl.when(i < 2)
    def _():
        def body(n, c):
            e, s = n % q, n // q
            for b in range(8):
                put(b, e, mult(geo.qr * s, 16), geo.qr, base + 24 * geo.qr * e + 8 * s + b, 24)
            return c

        lax.fori_loop(0, 3 * q, body, 0)

    def rows_part(a0, ro, shift, count):
        def body(n, c):
            e, bl = n % q, n // q
            bb = bl + shift
            for b in range(8):
                put(
                    bb % V,
                    e,
                    mult(ro + geo.ap * (bb // V) + geo.ho * b, 16),
                    geo.ho,
                    base + a0 + 8 * (128 * bl + geo.ho * e) + b,
                    8,
                )
            return c

        lax.fori_loop(0, count * q, body, 0)

    def cols_part(a0, nr, ro):
        def body(n, c):
            e, t = n % q, n // q
            for b in range(8):
                put(b, e, mult(ro + nr * t, 16), nr, base + a0 + 32 * nr * e + 8 * t + b, 32)
            return c

        lax.fori_loop(0, 4 * q, body, 0)

    @pl.when(i == 2)
    def _():
        rows_part(0, 0, 0, 8)
        cols_part(8192, geo.u2, geo.ap)

    @pl.when((i == 3) | (i == 4))
    def _():
        cols_part(0, geo.u3, 0)

    @pl.when(i == 5)
    def _():
        cols_part(0, geo.u2, 0)
        rows_part(4096, geo.bp, 0, 8)

    @pl.when(i >= 6)
    def _():
        rows_part(0, 0, 4 * (i - 6), 12)


def owner_moves(geo, i, j):
    k = i - 6
    return (
        (i < 6, 0, mult(geo.seg * i, 16), geo.seg),
        (i >= 6, mult(geo.ap * k, 16), mult(6 * geo.seg + 2 * geo.ap * k, 16), geo.ap),
        ((i >= 6) & (j // 4 == k), mult(geo.ap * (1 - k), 16), 6 * geo.seg + geo.ap, geo.ap),
    )


def sib_owner_rows(geo, sib, z_ref, sem):
    _, i, _ = geo.place()

    @pl.when(sib < 6)
    def _():
        arrive((z_ref, (slice(None), pl.ds(0, geo.seg))), sem)

    @pl.when((sib >= 6) & (i // 4 == sib - 6))
    def _():
        arrive((z_ref, (slice(None), pl.ds(0, 2 * geo.ap))), sem)

    @pl.when((sib >= 6) & (i // 4 != sib - 6))
    def _():
        arrive((z_ref, (slice(None), pl.ds(0, geo.ap))), sem)


def rot_tables(t):
    half = ROT // 2
    freq = (10000.0 ** (-2.0 * np.arange(half, dtype=np.float32) / ROT)).astype(np.float32)
    ang = np.arange(t, dtype=np.float32)[:, None] * freq[None, :]
    cos = np.ones((t, 128), np.float32)
    sin = np.zeros((t, 128), np.float32)
    for h in range(2):
        for k in range(2):
            lo = 64 * h + half * k
            cos[:, lo : lo + half] = np.cos(ang)
            sin[:, lo : lo + half] = np.sin(ang) * (1 if k else -1)
    return jnp.asarray(cos), jnp.asarray(sin)


def rot(v, cos, sin, lane, back):
    up = pltpu.roll(v, 120, 1)
    down = pltpu.roll(v, 8, 1)
    partner = jnp.where(lane % 16 < 8, up, down)
    turn = partner * sin
    return v * cos - turn if back else v * cos + turn


def main_kernel(
    geo, w_hbm, xin, gin, cos_ref, sin_ref, so_ref, sa_ref, f_hbm, tail_ref,
    buf, hb, e_ref, vs, z_ref, x_ref, g_ref, v_ref,
    vf, rowv, wq, wo, wu, wd, xh, n1, n2, qs, ks, vv, hid, du, ob, do, dqkv, dqs, acc, vp_ref, lse,
    rb_ref, rz, sibo, siba, rcvo, rcva, vr, vq, vsum, hbuf, lsem, ssem, rsem, csem, *spare,
):
    gz_ref = z_ref
    po_ref, fb = (g_ref, e_ref) if geo.tight else spare
    q, tl, t = geo.q, geo.tl, geo.t
    seg, ap, bp = geo.seg, geo.ap, geo.bp
    d, i, rho = geo.place()
    j = i
    z, c = i // 2, i % 2
    sib = 2 * z + 1 - c
    near = (None, d - d % 2 + (1 - d % 2), (d + 2) % 4, 3 - d)
    dev = partial(geo.dev, rho=rho)
    early = Sends(ssem, rsem)
    tx = early.group()
    lc = Sends(csem, None)
    whole = slice(None)

    def spread_one(tx, ok, part, sem):
        if geo.square:
            for k in (1, 2):
                tx.send(ok, part(d, None), part(d, None), sem + k - 1, dev(near[k], i))
        else:
            for k in range(1, q):
                tx.send(ok, part(d, None), part(d, None), sem + k - 1, dev((d + k) % q, i))

    def spread_two(tx, ok, part, sem):
        if geo.square:
            for k in (1, 2):
                Sends.when(ok, lambda: arrive(part(near[k], None), (rsem, sem + k - 1)))
                half = part(near[k], k - 1)
                tx.send(ok, half, half, sem + 1 + k, dev(near[3 - k], i))

    def spread_three(ok, part, sem):
        if geo.square:
            for k in (1, 2):
                Sends.when(ok, lambda: arrive(part(near[3], k - 1), (rsem, sem + 1 + k)))
        else:
            for k in range(1, q):
                Sends.when(ok, lambda: arrive(part((d + q - k) % q, None), (rsem, sem + k - 1)))

    load = pltpu.make_async_copy(w_hbm, buf.at[pl.ds(HEAD, OWN)], lsem.at[0])
    load.start()
    rows_own = pl.ds(mult(i * tl, 16), tl)
    own = [
        pltpu.make_async_copy(xin, x_ref.at[rows_own], lsem.at[1]),
        pltpu.make_async_copy(gin, g_ref.at[rows_own], lsem.at[2]),
    ]
    for cp in own:
        cp.start()
    entry_barrier(geo, d, i, rho)
    halo = pl.ds(OWN - 109, 109)
    early.send(i < V - 1, (w_hbm, halo), (hb, pl.ds(0, 109)), 0, dev(d, (i + 1) % V))

    def chain(a, src, ref):
        dst = (ref, rows_own)
        early.send(z < CHIPS - 1, src, dst, 4 + 6 * a, dev(d, (i + 2) % V))
        early.send(z > 0, src, dst, 7 + 6 * a, dev(d, (i + V - 2) % V))
        early.send(None, src, dst, 2 + a, dev(d, sib))

    def hop(a, ref, k):
        for s, sign in ((0, 1), (1, -1)):
            there = (z >= k + 1) if sign == 1 else (z + k + 1 < CHIPS)
            src_i = (i - 2 * sign * (k + 1) + 2 * V) % V
            rows = pl.ds(mult(src_i * tl, 16), tl)
            rs = 4 + 6 * a + 3 * s + k
            part = (ref, rows)

            @pl.when(there)
            def _():
                arrive(part, (rsem, rs))

            if k < CHIPS - 2:
                on = (z < CHIPS - 1) if sign == 1 else (z > 0)
                early.send(there & on, part, part, rs + 1, dev(d, (i + 2 * sign + V) % V))
            early.send(there, part, part, 2 + a, dev(d, sib))

    chain(0, xin, x_ref)
    load.wait()

    @pl.when(i > 0)
    def _():
        arrive((hb, pl.ds(0, 109)), (rsem, 0))
        buf[pl.ds(HEAD - 104, 104), :] = hb[pl.ds(5, 104), :]

    @pl.when(i == V - 1)
    def _():
        vs[...] = buf[pl.ds(HEAD + OWN - VECS, VECS), :].astype(BF16)
        v_ref[...] = vs[...]

    cut_share(geo, i, buf, e_ref)

    def slices_to(k):
        tx = early.group()
        for cc in range(2):
            to = (2 * (z + k) + cc) % V
            for ok, erow, zrow, n in owner_moves(geo, i, to):
                src = (e_ref, (to, d, pl.ds(erow, n)))
                tx.send(ok, src, (z_ref, (d, pl.ds(zrow, n))), 16 + k, dev(d, to))
        return tx

    def slices_of(k):
        base = ((z + CHIPS - k) % CHIPS) * 2 * seg

        def part(e, half):
            at, n = (base, 2 * seg) if half is None else (base + half * seg, seg)
            return (z_ref, (e, pl.ds(mult(at, 16), n)))

        return None, part, SPREAD + geo.ss * (k - 1)

    first = slices_to(1)
    for k in range(1, V):
        early.send(i == V - 1, vs, v_ref, 1, dev(d, (i + k) % V))
    for ok, erow, zrow, n in owner_moves(geo, i, sib):
        src = (e_ref, (sib, whole, pl.ds(erow, n)))
        early.send(ok, src, (z_ref, (whole, pl.ds(zrow, n))), 16, dev(d, sib))
    for ok, erow, zrow, n in owner_moves(geo, i, i):
        lc.copy(ok, (e_ref, (i, whole, pl.ds(erow, n))), (z_ref, (whole, pl.ds(zrow, n))))
    first.finish()
    second = slices_to(2)
    arrive((z_ref, (0, pl.ds(0, 2 * seg))), (rsem, 17))
    spread_one(early, *slices_of(1))
    second.finish()
    third = slices_to(3)
    arrive((z_ref, (0, pl.ds(0, 2 * seg))), (rsem, 18))
    spread_one(early, *slices_of(2))
    third.finish()
    hop(0, x_ref, 0)
    arrive((z_ref, (0, pl.ds(0, 2 * seg))), (rsem, 19))
    spread_one(early, *slices_of(3))
    spread_two(early, *slices_of(1))
    hop(0, x_ref, 1)
    chain(1, gin, g_ref)
    spread_two(early, *slices_of(2))
    hop(0, x_ref, 2)
    for cp in own:
        cp.wait()

    @pl.when(i < V - 1)
    def _():
        arrive(v_ref, (rsem, 1))

    nrb = t // RB
    vf[...] = v_ref[...].astype(F32)
    for k in range(9):
        for b in range(8):
            rowv[k : k + 1, 128 * b : 128 * b + 128] = vf[8 * k + b : 8 * k + b + 1, :]
    acc[...] = jnp.zeros_like(acc)
    vp_ref[...] = jnp.zeros_like(vp_ref)
    gp = lambda b, r: pl.ds(mult(b * t + r * RB, RB), RB)
    kv0, kv1 = 4 * t, 5 * t
    buf[kv0 : kv0 + 2 * t, :] = jnp.zeros((2 * t, 128), F32)

    def rb_of(r):
        return pl.ds(mult(r * RB, RB), RB)

    lane = lax.broadcasted_iota(jnp.int32, (RB, 128), 1)
    arrive((x_ref, pl.ds(0, CHIPS * tl)), (rsem, 2))

    def norms(r, carry):
        rb = rb_of(r)
        x = x_ref[rb, :].astype(F32)
        mean = jnp.mean(x, axis=1, keepdims=True)
        mid = x - mean
        var = jnp.mean(mid * mid, axis=1, keepdims=True)
        inv = lax.rsqrt(var + 1e-05)
        xhat = mid * inv
        xh[rb, 0:1] = mean
        xh[rb, 1:2] = inv
        n1[rb, :] = (xhat * rowv[0:1, :] + rowv[1:2, :]).astype(BF16)
        n2[rb, :] = (xhat * rowv[2:3, :] + rowv[3:4, :]).astype(BF16)
        return carry

    lax.fori_loop(0, nrb, norms, 0)
    spread_two(early, *slices_of(3))
    hop(1, g_ref, 0)
    sib_owner_rows(geo, sib, z_ref, (rsem, 16))
    lc.finish()
    for k in range(1, CHIPS):
        spread_three(*slices_of(k))
    mats = (wq, wo, wu, wd)
    for e, zrow, n, m, row, ln in geo.maps():
        mats[m][row : row + n, ln : ln + 128] = z_ref[e, zrow : zrow + n, :]
    hop(1, g_ref, 1)

    def forward(r, carry):
        rb = rb_of(r)
        qkv = dot(n1[rb, :], wq[...])
        cos, sin = cos_ref[rb, :], sin_ref[rb, :]
        qh = qkv[:, 0:128] + vf[pl.ds(32 + j, 1), :]
        kh = qkv[:, 128:256] + vf[pl.ds(40 + j, 1), :]
        vh = qkv[:, 256:384] + vf[pl.ds(48 + j, 1), :]
        qs[rb, :] = (rot(qh, cos, sin, lane, False) * 0.125).astype(BF16)
        ks[rb, :] = rot(kh, cos, sin, lane, False).astype(BF16)
        vv[rb, :] = vh.astype(BF16)
        up = dot(n2[rb, :], wu[...])
        for b in range(4):
            cols = slice(128 * b, 128 * b + 128)
            u = up[:, cols] + vf[pl.ds(72 + 8 * b + j, 1), :]
            phi = 0.5 + 0.5 * lax.erf(u * (1.0 / math.sqrt(2.0)))
            hid[rb, cols] = (u * phi).astype(BF16)
            buf[gp(b, r), :] = phi + u * (jnp.exp(-0.5 * u * u) * (1.0 / math.sqrt(2.0 * math.pi)))
        return carry

    lax.fori_loop(0, nrb, forward, 0)
    hop(1, g_ref, 2)

    ra = geo.rba
    left = lax.broadcasted_iota(jnp.int32, (ra, 128), 1) < 64
    diag = lax.broadcasted_iota(jnp.int32, (ra, ra), 0) >= lax.broadcasted_iota(jnp.int32, (ra, ra), 1)
    zero = jnp.zeros((), BF16)

    def mine(h, v):
        return jnp.where(left if h == 0 else jnp.logical_not(left), v, zero)

    def scores(r, qm):
        n = (r + 1) * ra
        s = dot_nt(qm, ks[0:n, :])
        tail = jnp.where(diag, s[:, n - ra : n], -1e30)
        return tail if r == 0 else jnp.concatenate([s[:, : n - ra], tail], axis=1)

    for r in range(t // ra):
        rb, n = slice(r * ra, r * ra + ra), (r + 1) * ra
        outs = []
        for h in range(2):
            s = scores(r, mine(h, qs[rb, :]))
            top = jnp.max(s, axis=1, keepdims=True)
            ex = jnp.exp(s - top)
            tot = jnp.sum(ex, axis=1, keepdims=True)
            lse[rb, h : h + 1] = top + jnp.log(tot)
            outs.append(dot((ex * (1.0 / tot)).astype(BF16), vv[0:n, :]))
        ob[rb, :] = jnp.where(left, outs[0], outs[1]).astype(BF16)

    def outputs(r, carry):
        rb = rb_of(r)
        po_ref[rb, :] = (dot(hid[rb, :], wd[...]) + dot(ob[rb, :], wo[...])).astype(BF16)
        return carry

    def to_sibling(a, part, sums):
        for k in range(CHIPS):
            rows = pl.ds(mult((2 * k + 1 - c) * tl, 16), tl)
            tx.send(None, (part, rows), (sums, k), 20 + a, dev(d, sib))

    def to_line(a, part, sums, got):
        arrive(sums, (rsem, 20 + a))
        for k in range(CHIPS):
            rows = pl.ds(mult((2 * k + c) * tl, 16), tl)
            sums[k] = (part[rows, :].astype(F32) + sums[k].astype(F32)).astype(BF16)
        for k in range(1, CHIPS):
            to = (z + k) % CHIPS
            tx.send(None, (sums, to), (got, k - 1), 22 + a, dev(d, 2 * to + c))

    if not geo.tight:
        lax.fori_loop(0, nrb, outputs, 0)
        to_sibling(0, po_ref, sibo)
    arrive((g_ref, pl.ds(0, CHIPS * tl)), (rsem, 3))

    def back_mlp(r, carry):
        rb = rb_of(r)
        g = g_ref[rb, :]
        dh = dot_nt(g, wd[...])
        for b in range(4):
            cols = slice(128 * b, 128 * b + 128)
            low = (dh[:, cols] * buf[gp(b, r), :]).astype(BF16)
            du[rb, cols] = low
            acc[5:6, cols] += jnp.sum(low.astype(F32), axis=0, keepdims=True)
        do[rb, :] = dot_nt(g, wo[...]).astype(BF16)
        acc[4:5, :] += jnp.sum(g.astype(F32), axis=0, keepdims=True)
        return carry

    lax.fori_loop(0, nrb, back_mlp, 0)
    early.finish()
    pc = 4096 // q
    ph = pc // 2

    def grad_down(k, carry):
        res = dot_tn(hid[:, pl.ds(mult(k * 256, 256), 256)], g_ref[...]).astype(BF16)
        for h in range(2):
            row = 5 * seg + bp + ap * (2 * k + h)
            for e in range(q):
                for b in range(8):
                    r0 = 128 * h + geo.ho * e
                    block = res[r0 : r0 + geo.ho, 128 * b : 128 * b + 128]
                    gz_ref[e, pl.ds(mult(row + geo.ho * b, 16), geo.ho), :] = block
        return carry

    def grad_cols(left_ref, right_ref, out, blocks):
        def body(k, carry):
            cols = pl.ds(mult(k * 256, 256), 256)
            out[cols, :] = dot_tn(left_ref[:, cols], right_ref[...]).astype(BF16)
            return carry

        lax.fori_loop(0, blocks, body, 0)

    def pack(which):
        for e, zrow, n, m, row, ln in geo.maps():
            if m in which:
                gz_ref[e, zrow : zrow + n, :] = mats[m][row : row + n, ln : ln + 128]

    def halves(p, h):
        return pl.ds(p * pc + h * ph, ph), pl.ds(p * ph, ph)

    def sum_one(p):
        sem = SUMS + geo.ss * p
        if geo.square:
            for k in (1, 2):
                rows, at = halves(p, k - 1)
                for slot, e in enumerate((near[k], near[3])):
                    dst = (rb_ref, (2 * (k - 1) + slot, at))
                    tx.send(None, (gz_ref, (e, rows)), dst, sem + k - 1, dev(near[k], i))
        else:
            rows = pl.ds(p * pc, pc)
            for k in range(1, q):
                e = (d + k) % q
                tx.send(None, (gz_ref, (e, rows)), (rb_ref, (k - 1, rows)), sem + k - 1, dev(e, i))

    def sum_two(p):
        sem = SUMS + geo.ss * p
        if geo.square:
            for k in (1, 2):
                rows, at = halves(p, k - 1)
                arrive((rb_ref, (pl.ds(2 * (k - 1), 2), at)), (rsem, sem + k - 1))
                mid = 2 * (k - 1) + 1
                tot = gz_ref[near[3 - k], rows, :].astype(F32) + rb_ref[mid, at, :].astype(F32)
                rb_ref[mid, at, :] = tot.astype(BF16)
                tx.send(None, (rb_ref, (mid, at)), (rb_ref, (3 + k, at)), sem + 1 + k, dev(near[3 - k], i))

    def sum_three(p):
        sem = SUMS + geo.ss * p
        if geo.square:
            for k in (1, 2):
                rows, at = halves(p, k - 1)
                arrive((rb_ref, (3 + k, at)), (rsem, sem + 1 + k))
                tot = gz_ref[d, rows, :].astype(F32) + rb_ref[2 * (k - 1), at, :].astype(F32)
                rz[rows, :] = (tot + rb_ref[3 + k, at, :].astype(F32)).astype(BF16)
        else:
            rows = pl.ds(p * pc, pc)
            for k in range(1, q):
                arrive((rb_ref, (k - 1, rows)), (rsem, sem + k - 1))
            tot = gz_ref[d, rows, :].astype(F32)
            for k in range(q - 1):
                tot = tot + rb_ref[k, rows, :].astype(F32)
            rz[rows, :] = tot.astype(BF16)

    moves = (
        ((0, 0, 0, seg, 0), (1, seg, 0, seg, 0), (2, 2 * seg, 0, ap, 0)),
        (
            (2, 2 * seg + ap, ap, bp, 1),
            (3, 3 * seg, 0, seg, 1),
            (4, 4 * seg, 0, seg, 1),
            (5, 5 * seg, 0, bp, 1),
        ),
        ((5, 5 * seg + bp, bp, ap, 2), (6, 6 * seg, 0, ap, 2), (7, 6 * seg + 2 * ap, ap, ap, 2)),
    )

    def to_owners(p):
        sum_three(p)
        for o, zrow, frow, n, kind in moves[p]:
            src, dst = (rz, pl.ds(zrow, n)), (fb, (i, d, pl.ds(frow, n)))
            tx.send(i != o, src, dst, 27 + kind, dev(d, o))
            lc.copy(i == o, src, dst)
        if p == 2:
            for o in (6, 7):
                here = i // 4 == o - 6
                src, dst = (rz, pl.ds(6 * seg + ap, ap)), (fb, (i, d, pl.ds(ap * (7 - o), ap)))
                tx.send(here & (i != o), src, dst, 30, dev(d, o))
                lc.copy(here & (i == o), src, dst)

    def held(p):
        out = [(o, 0, V, V - 1, frow, n, kind) for o, _, frow, n, kind in moves[p]]
        if p == 2:
            out += [(6, 0, 4, 4, ap, ap, 3), (7, 4, 4, 3, 0, ap, 3)]
        return out

    def held_part(j0, js, frow, n):
        def part(e, half):
            at, m = (j0, js) if half is None else (j0 + half * (js // 2), js // 2)
            return (fb, (pl.ds(at, m), e, pl.ds(frow, n)))

        return part

    def plane(p, stage):
        if stage == 1:
            lc.finish()
        for o, j0, js, remote, frow, n, kind in held(p):
            ok, part, sem = i == o, held_part(j0, js, frow, n), SPREAD + geo.ss * (3 + kind)
            if stage == 1:
                Sends.when(ok, lambda: arrive((fb, (pl.ds(0, remote), 0, pl.ds(frow, n))), (rsem, 27 + kind)))
                spread_one(tx, ok, part, sem)
            elif stage == 2:
                spread_two(tx, ok, part, sem)
            else:
                spread_three(ok, part, sem)

    lax.fori_loop(0, 2, grad_down, 0)
    sum_one(2)
    if not geo.tight:
        to_line(0, po_ref, sibo, rcvo)

    for r in range(t // ra):
        rb, n = slice(r * ra, r * ra + ra), (r + 1) * ra
        dqh = []
        for h in range(2):
            qm, gm = mine(h, qs[rb, :]), mine(h, do[rb, :])
            prob = jnp.exp(scores(r, qm) - lse[rb, h : h + 1])
            dp = dot_nt(gm, vv[0:n, :])
            delta = jnp.sum(prob * dp, axis=1, keepdims=True)
            ds = (prob * (dp - delta)).astype(BF16)
            dqh.append(dot(ds, ks[0:n, :]))
            buf[kv0 : kv0 + n, :] += dot_tn(ds, qm)
            buf[kv1 : kv1 + n, :] += dot_tn(prob.astype(BF16), gm)
        dqs[rb, :] = jnp.where(left, dqh[0], dqh[1])

    sum_two(2)

    def back(r, carry):
        rb = rb_of(r)
        cos, sin = cos_ref[rb, :], sin_ref[rb, :]
        low = jnp.concatenate(
            [
                (rot(dqs[rb, :], cos, sin, lane, True) * 0.125).astype(BF16),
                rot(buf[pl.ds(mult(kv0 + r * RB, RB), RB), :], cos, sin, lane, True).astype(BF16),
                buf[pl.ds(mult(kv1 + r * RB, RB), RB), :].astype(BF16),
            ],
            axis=1,
        )
        dqkv[rb, :] = low
        acc[6:7, 0:384] += jnp.sum(low.astype(F32), axis=0, keepdims=True)
        xhat = (x_ref[rb, :].astype(F32) - xh[rb, 0:1]) * xh[rb, 1:2]
        d1 = dot_nt(low, wq[...])
        acc[0:1, :] += jnp.sum(d1 * xhat, axis=0, keepdims=True)
        acc[1:2, :] += jnp.sum(d1, axis=0, keepdims=True)
        d2 = dot_nt(du[rb, :], wu[...])
        acc[2:3, :] += jnp.sum(d2 * xhat, axis=0, keepdims=True)
        acc[3:4, :] += jnp.sum(d2, axis=0, keepdims=True)
        x_ref[rb, :] = (d1 * rowv[0:1, :] + d2 * rowv[2:3, :]).astype(BF16)
        return carry

    lax.fori_loop(0, nrb, back, 0)
    to_sibling(1, x_ref, siba)
    res = dot_tn(ob[...], g_ref[...]).astype(BF16)
    for e in range(q):
        for b in range(8):
            row = 2 * seg + geo.ho * b
            gz_ref[e, row : row + geo.ho, :] = res[geo.ho * e : geo.ho * e + geo.ho, 128 * b : 128 * b + 128]
    if geo.tight:
        lax.fori_loop(0, nrb, outputs, 0)
        to_sibling(0, po_ref, sibo)
    grad_cols(n1, dqkv, wq, 4)
    pack((0,))
    sum_one(0)
    to_owners(2)
    grad_cols(n2, du, wu, 4)
    pack((2,))
    sum_one(1)
    sum_two(0)
    if geo.tight:
        to_line(0, po_ref, sibo, rcvo)
    to_line(1, x_ref, siba, rcva)
    plane(2, 1)
    zeroth = jnp.where(j == 0, 1.0, 0.0)
    for b in range(8):
        cols = slice(128 * b, 128 * b + 128)
        for k in range(4):
            vp_ref[8 * k + b : 8 * k + b + 1, :] = acc[k : k + 1, cols]
        for k in (7, 8):
            vp_ref[8 * k + b : 8 * k + b + 1, :] = acc[4:5, cols] * zeroth
    for k in range(3):
        vp_ref[pl.ds(32 + 8 * k + j, 1), :] = acc[6:7, 128 * k : 128 * k + 128]
    for k in range(4):
        vp_ref[pl.ds(72 + 8 * k + j, 1), :] = acc[5:6, 128 * k : 128 * k + 128]
    tx.send(i < V - 1, vp_ref, (vr, i), 24, dev(d, V - 1))
    to_owners(0)
    sum_two(1)
    plane(2, 2)
    plane(0, 1)
    to_owners(1)
    plane(0, 2)
    plane(1, 1)
    for a, (sums, got, out) in enumerate(((sibo, rcvo, so_ref), (siba, rcva, sa_ref))):
        arrive(got, (rsem, 22 + a))
        tot = sums[z].astype(F32)
        for k in range(CHIPS - 1):
            tot = tot + got[k].astype(F32)
        if a == 0:
            tot = tot + (rowv[7:8, :] + rowv[8:9, :])
        out[...] = tot

    def head_rows(jj, row, n, stride, s):
        for b in range(8):
            at = row if jj is None else row + n * b
            src = fb[b if jj is None else jj, 0, at : at + 16, :]
            hbuf[pl.ds(8 * s + b, 16, stride=stride), :] = src.astype(F32)

    @pl.when((d == 0) & (i == 1))
    def _():
        for s in range(3):
            head_rows(None, geo.qr * s, geo.qr, 24, s)

    for o, n in ((3, geo.u3), (4, geo.u3), (5, geo.u2)):
        @pl.when((d == 0) & (i == o))
        def _():
            for s in range(4):
                head_rows(None, n * s, n, 32, s)

    for o, jj in ((2, 0), (6, 0), (7, 4)):
        @pl.when((d == 0) & (i == o))
        def _():
            head_rows(jj, 0, geo.ho, 8, 0)

    for e in range(q):
        to = dev(e, (i + V - 1) % V)
        tx.send((d == 0) & (i > 0), (hbuf, pl.ds(0, VECS)), tail_ref, 26, to)

    @pl.when(i == V - 1)
    def _():
        arrive((vr, pl.ds(0, V - 1)), (rsem, 24))
        tot = vp_ref[...]
        for k in range(V - 1):
            tot = tot + vr[k]
        vsum[...] = tot

    for k in range(1, q):
        tx.send(i == V - 1, vsum, (vq, k - 1), 25, dev((d + k) % q, i))
    plane(1, 2)

    @pl.when(i == V - 1)
    def _():
        arrive(vq, (rsem, 25))
        tot = vsum[...]
        for k in range(q - 1):
            tot = tot + vq[k]
        tail_ref[...] = tot

    @pl.when(i < V - 1)
    def _():
        arrive(tail_ref, (rsem, 26))

    for p in (2, 0, 1):
        plane(p, 3)
    tx.finish()
    out = pltpu.make_async_copy(fb, f_hbm, lsem.at[3])
    out.start()
    out.wait()


def main(geo, w, x, g):
    q, tl, t = geo.q, geo.tl, geo.t
    vm = pl.BlockSpec(memory_space=pltpu.VMEM)
    hbm = pl.BlockSpec(memory_space=pl.ANY)
    cos, sin = rot_tables(t)
    line = pltpu.VMEM((CHIPS, tl, D), BF16)
    line3 = pltpu.VMEM((CHIPS - 1, tl, D), BF16)
    vec = pltpu.VMEM((VECS, 128), F32)
    low = lambda *dims: pltpu.VMEM(dims, BF16)
    full = lambda *dims: pltpu.VMEM(dims, F32)
    return pl.pallas_call(
        partial(main_kernel, geo),
        out_shape=(
            jax.ShapeDtypeStruct((tl, D), F32),
            jax.ShapeDtypeStruct((tl, D), F32),
            jax.ShapeDtypeStruct((V, q, geo.er, 128), BF16),
            jax.ShapeDtypeStruct((VECS, 128), F32),
        ),
        in_specs=[hbm, hbm, hbm, vm, vm],
        out_specs=(vm, vm, hbm, vm),
        scratch_shapes=[
            full(HEAD + OWN + 3, 128),
            full(112, 128),
            low(V, q, geo.er, 128),
            low(VECS, 128),
            low(q, geo.zr, 128),
            low(t, D),
            low(t, D),
            low(VECS, 128),
            vec,
            full(16, D),
            low(D, 384),
            low(128, D),
            low(D, 512),
            low(512, D),
            full(t, 2),
            low(t, D),
            low(t, D),
            low(t, 128),
            low(t, 128),
            low(t, 128),
            low(t, 512),
            low(t, 512),
            low(t, 128),
            low(t, 128),
            low(t, 384),
            full(t, 128),
            full(8, D),
            vec,
            full(t, 2),
            low(6, geo.zr // 2, 128) if geo.square else low(q - 1, geo.zr, 128),
            low(geo.zr, 128),
            line, line, line3, line3,
            full(V - 1, VECS, 128),
            full(q - 1, VECS, 128),
            vec,
            full(512, 128),
            pltpu.SemaphoreType.DMA((4,)),
            pltpu.SemaphoreType.DMA((400,)),
            pltpu.SemaphoreType.DMA((SUMS + 3 * geo.ss,)),
            pltpu.SemaphoreType.DMA((24,)),
        ] + ([] if geo.tight else [low(t, D), low(V, q, geo.er, 128)]),
        compiler_params=pltpu.CompilerParams(
            collective_id=0, has_side_effects=True, vmem_limit_bytes=63 << 20
        ),
        name="layer",
    )(w, x, g, cos, sin)


def adam_kernel(
    geo, so_ref, sa_ref, x_ref, g_ref, tail_ref, f_hbm, w_hbm, m_hbm, s_hbm,
    lo_ref, tg_ref, wg_hbm, nw_hbm, nm_hbm, ns_hbm, wb, mb, sb, ob, gb, fb, lsem,
):
    _, i, _ = geo.place()
    loads = [pltpu.make_async_copy(f_hbm, fb, lsem.at[0])]
    for k, (h, b) in enumerate(((w_hbm, wb), (m_hbm, mb), (s_hbm, sb))):
        loads.append(pltpu.make_async_copy(h, b.at[pl.ds(0, OWN)], lsem.at[k + 1]))
    for ld in loads:
        ld.start()
    x = x_ref[...].astype(F32)
    sa = sa_ref[...]
    lo_ref[...] = (x + so_ref[...]).astype(BF16)
    mid = x - jnp.mean(x, axis=1, keepdims=True)
    inv = lax.rsqrt(jnp.mean(mid * mid, axis=1, keepdims=True) + 1e-05)
    xhat = mid * inv
    dx = inv * (sa - jnp.mean(sa, axis=1, keepdims=True) - xhat * jnp.mean(sa * xhat, axis=1, keepdims=True))
    tg_ref[...] = g_ref[...].astype(F32) + dx
    gb[pl.ds(ALI, VECS), :] = tail_ref[...]
    loads[0].wait()
    paste_share(geo, i, gb, fb)
    for ld in loads[1:]:
        ld.wait()
    rows_n = 1024
    full = OWN // rows_n
    pairs = ((wg_hbm, ob), (nw_hbm, wb), (nm_hbm, mb), (ns_hbm, sb))

    def adam(n, carry):
        rows = pl.ds(mult(n * rows_n, rows_n), rows_n)
        adam_rows(i, rows, n * rows_n, rows_n, wb, mb, sb, ob, gb)
        for k, (h, b) in enumerate(pairs):
            pltpu.make_async_copy(b.at[rows], h.at[rows], lsem.at[4 + k]).start()
        return carry

    lax.fori_loop(0, full, adam, 0)
    rest = OWN - full * rows_n
    adam_rows(i, pl.ds(full * rows_n, 16), full * rows_n, 16, wb, mb, sb, ob, gb)
    for k, (h, b) in enumerate(pairs):
        rows = pl.ds(full * rows_n, rest)
        pltpu.make_async_copy(b.at[rows], h.at[rows], lsem.at[4 + k]).start()
    for k, (h, b) in enumerate(pairs):
        pltpu.make_async_copy(b.at[pl.ds(0, OWN)], h, lsem.at[4 + k]).wait()


def adam_rows(i, rows, start, n, wb, mb, sb, ob, gb):
    g = gb[pl.ds(13 * i + start, n), :]
    w = wb[rows, :]
    m = BETA_ONE * mb[rows, :] + (1.0 - BETA_ONE) * g
    s = BETA_TWO * sb[rows, :] + (1.0 - BETA_TWO) * g * g
    ob[rows, :] = g
    mb[rows, :] = m
    sb[rows, :] = s
    mh = m * (1.0 / (1.0 - BETA_ONE**STEP))
    vh = s * (1.0 / (1.0 - BETA_TWO**STEP))
    wb[rows, :] = w - LEARN_RATE * (mh / (jnp.sqrt(vh) + EPSILON) + DECAY_RATE * w)


def paste_share(geo, i, gb, f_ref):
    q = geo.q

    def put(j, e, row, n, start, stride):
        gb[pl.ds(start, n, stride=stride), :] = f_ref[j, e, pl.ds(row, n), :].astype(F32)

    @pl.when(i < 2)
    def _():
        def body(n, c):
            e, s = n % q, n // q
            for b in range(8):
                put(b, e, mult(geo.qr * s, 16), geo.qr, 24 * geo.qr * e + 8 * s + b, 24)
            return c

        lax.fori_loop(0, 3 * q, body, 0)

    def rows_part(a0, ro, shift, count):
        def body(n, c):
            e, bl = n % q, n // q
            bb = bl + shift
            for b in range(8):
                put(
                    bb % V,
                    e,
                    mult(ro + geo.ap * (bb // V) + geo.ho * b, 16),
                    geo.ho,
                    a0 + 8 * (128 * bl + geo.ho * e) + b,
                    8,
                )
            return c

        lax.fori_loop(0, count * q, body, 0)

    def cols_part(a0, nr, ro):
        def body(n, c):
            e, t = n % q, n // q
            for b in range(8):
                put(b, e, mult(ro + nr * t, 16), nr, a0 + 32 * nr * e + 8 * t + b, 32)
            return c

        lax.fori_loop(0, 4 * q, body, 0)

    @pl.when(i == 2)
    def _():
        rows_part(0, 0, 0, 8)
        cols_part(8192, geo.u2, geo.ap)

    @pl.when((i == 3) | (i == 4))
    def _():
        cols_part(0, geo.u3, 0)

    @pl.when(i == 5)
    def _():
        cols_part(0, geo.u2, 0)
        rows_part(4096, geo.bp, 0, 8)

    @pl.when(i >= 6)
    def _():
        rows_part(0, 0, 4 * (i - 6), 12)


def adam(geo, so, sa, x, g, tail, f, w, m, s):
    tl = geo.tl
    vm = pl.BlockSpec(memory_space=pltpu.VMEM)
    hbm = pl.BlockSpec(memory_space=pl.ANY)
    flat = jax.ShapeDtypeStruct((OWN, 128), F32)
    big = pltpu.VMEM((OWN + 3, 128), F32)
    return pl.pallas_call(
        partial(adam_kernel, geo),
        out_shape=(
            jax.ShapeDtypeStruct((tl, D), BF16),
            jax.ShapeDtypeStruct((tl, D), F32),
            flat, flat, flat, flat,
        ),
        in_specs=[vm] * 5 + [hbm] * 4,
        out_specs=(vm, vm, hbm, hbm, hbm, hbm),
        scratch_shapes=[
            big, big, big, big,
            pltpu.VMEM((ALI + 128, 128), F32),
            pltpu.VMEM((V, geo.q, geo.er, 128), BF16),
            pltpu.SemaphoreType.DMA((8,)),
        ],
        compiler_params=pltpu.CompilerParams(vmem_limit_bytes=50 << 20),
        name="adam",
    )(so, sa, x, g, tail, f, w, m, s)


def local(mesh, tokens, cotangent, weights, first_moment, second_moment):
    rep = mesh.shape["ctx"] // V
    rows = tokens.shape[1]
    x, g = tokens[0], cotangent[0]
    flats = [weights, first_moment, second_moment]
    if rep > 1:
        groups = [[rep * k + r for r in range(rep)] for k in range(V)]
        join = lambda a: lax.all_gather(a, "ctx", axis=0, axis_index_groups=groups, tiled=True)
        x, g = join(x), join(g)
        flats = [join(a) for a in flats]
    w, m, s = [a.reshape(OWN, 128) for a in flats]
    geo = Geo(mesh, x.shape[0] * V)
    so, sa, f, tail = main(geo, w, x, g)
    outs = list(adam(geo, so, sa, x, g, tail, f, w, m, s))
    outs[2:] = [a.reshape(-1) for a in outs[2:]]
    if rep > 1:
        r = lax.axis_index("ctx") % rep
        outs = [lax.dynamic_slice_in_dim(a, r * (a.shape[0] // rep), a.shape[0] // rep, 0) for a in outs]
    return (outs[0][None], outs[1][None], *outs[2:])


def solution(mesh):
    return jax.shard_map(
        partial(local, mesh),
        mesh=mesh,
        in_specs=(P("dp", "ctx", None), P("dp", "ctx", None), P("ctx"), P("ctx"), P("ctx")),
        out_specs=(P("dp", "ctx", None), P("dp", "ctx", None), P("ctx"), P("ctx"), P("ctx"), P("ctx")),
        check_vma=False,
    )
```

time: 262 us -> 186 us (0.71)
  the two profiles are of different devices: /device:TPU:17 before, /device:TPU:15 now
where the time goes in v2:
time: 186 us; the launch traced here: 185 us
  Pallas kernels  181 us (97%)
  local copies, waits for them, and re-layouts  2.89 us (2%)
    pallas_call x1, Pallas kernels, main(): pl.pallas_call(partial(main_kernel, geo), out_shape=(jax.ShapeDtypeStruct...  163 us
    pallas_call x1, Pallas kernels, adam(): pl.pallas_call(partial(adam_kernel, geo), out_shape=(jax.ShapeDtypeStruct...  18.2 us

profile of v2, /device:TPU:15, one launch (start us, length us, event | category | flops | bytes accessed | tf_op | source)
XLA Modules:
  0.0 185.1 jit_solution(17056857257136819738)
XLA Ops:
  0.6 0.0 copy-start.1
  0.6 0.0 copy-start
  0.7 163.2 %layer.1 = (f32[128,1024]{1,0:T(8,128)}, f32[128,1024]{1,0:T(8,128)}, bf16[8,4,512,128]{3,2,1,0:T(8,128)(2,1)}, f32[104,128]{1,0:T(8,128)}) custom-call(f32[12301,128]{1,0:T(8,128)} %bitcast.15, bf16[128,1024]{1,0:T(8,128)(2,1)} %bitcast.11, bf16[128,1024]{1,0:T(8,128)(2,1)} %bitcast.13, f32[1024,128]{1,0:T(8,128)} %constant.4.clone.cos_ref, ...), custom_call_target="tpu_custom_call" | custom-call | tf_op jit(solution)/shard_map/layer/pallas_call | solution.py:838
  163.8 0.0 copy-done.1
  163.8 0.0 copy-done
  163.8 0.0 copy-start.2
  163.8 1.0 copy-done.2
  164.9 0.0 copy-start.3
  164.9 1.0 copy-done.3
  165.9 0.0 copy-start.4
  165.9 0.8 copy-done.4
  166.7 18.2 %adam.1 = (bf16[128,1024]{1,0:T(8,128)(2,1)}, f32[128,1024]{1,0:T(8,128)}, f32[12301,128]{1,0:T(8,128)}, f32[12301,128]{1,0:T(8,128)}, f32[12301,128]{1,0:T(8,128)}, /*index=5*/f32[12301,128]{1,0:T(8,128)}) custom-call(f32[128,1024]{1,0:T(8,128)S(1)} %copy-done.2, f32[128,1024]{1,0:T(8,128)S(1)} %copy-done.3, bf16[128,1024]{1,0:T(8,128)(2,1)S(1)} %bitcast.12, ...), custom_call_target="tpu_custom_call" | custom-call | tf_op jit(solution)/shard_map/adam/pallas_call | solution.py:1021
Async XLA Ops:
  0.6 163.2 %copy-start.1 = (bf16[1,128,1024]{2,1,0:T(8,128)(2,1)S(1)}, bf16[1,128,1024]{2,1,0:T(8,128)(2,1)}, u32[]{:S(2)}) copy-start(bf16[1,128,1024]{2,1,0:T(8,128)(2,1)} %param.8) | copy-start | bytes 786436
  0.6 163.2 %copy-start = (bf16[1,128,1024]{2,1,0:T(8,128)(2,1)S(1)}, bf16[1,128,1024]{2,1,0:T(8,128)(2,1)}, u32[]{:S(2)}) copy-start(bf16[1,128,1024]{2,1,0:T(8,128)(2,1)} %param.7) | copy-start | bytes 786436
  163.8 1.0 copy-start.2
  164.9 1.0 copy-start.3
  165.9 0.8 copy-start.4

commit v3 on v2

--- a/solution.py
+++ b/solution.py
@@ -31,8 +31,8 @@
 VECS = 104
 HEAD = 112
 RB = 256
-SPREAD = 31
-SUMS = 80
+PARTS = 29
+SPREAD = 45
 
 
 class Geo:
@@ -55,6 +55,8 @@
         self.rba = RB // 2 if self.tight else RB
         self.square = q == 4
         self.ss = max(4, q - 1)
+        self.sums = SPREAD + 19 * self.ss
+        self.lines = self.sums + 3 * self.ss
 
     def place(self):
         d = lax.axis_index("dp")
@@ -63,6 +65,14 @@
 
     def dev(self, e, j, rho):
         return {"dp": e, "ctx": j * self.rep + rho}
+
+    def up_parts(self):
+        return (
+            (0, self.u2, 2 * self.seg + self.ap),
+            (128, self.u3, 3 * self.seg),
+            (512, self.u3, 4 * self.seg),
+            (896, self.u2, 5 * self.seg),
+        )
 
     def maps(self):
         q, out = self.q, []
@@ -72,13 +82,7 @@
                     out.append((e, self.seg * i + self.qr * s, self.qr, 0, 512 * i + self.qr * e, 128 * s))
             for b in range(8):
                 out.append((e, 2 * self.seg + self.ho * b, self.ho, 1, self.ho * e, 128 * b))
-            parts = (
-                (0, self.u2, 2 * self.seg + self.ap),
-                (128, self.u3, 3 * self.seg),
-                (512, self.u3, 4 * self.seg),
-                (896, self.u2, 5 * self.seg),
-            )
-            for r0, nr, off in parts:
+            for r0, nr, off in self.up_parts():
                 for t in range(4):
                     out.append((e, off + nr * t, nr, 2, r0 + nr * e, 128 * t))
             for t in range(4):
@@ -121,26 +125,37 @@
 
 class Sends:
     def __init__(self, ssem, rsem, used=None):
-        self.ssem, self.rsem, self.used, self.open = ssem, rsem, used or [0], []
+        self.ssem, self.rsem, self.open = ssem, rsem, []
+        self.used = {} if used is None else used
 
     def group(self):
         return Sends(self.ssem, self.rsem, self.used)
 
-    def slot(self):
-        self.used[0] += 1
-        return (self.ssem, self.used[0] - 1)
-
-    def send(self, cond, src, dst, rs, dev):
-        slot = self.slot()
+    def slot(self, key):
+        return (self.ssem, self.used.setdefault(key or ("own", len(self.used)), len(self.used)))
+
+    def send(self, cond, src, dst, rs, dev, key=None):
+        slot = self.slot(key)
         make = lambda: rcopy(src, dst, slot, (self.rsem, rs), dev)
         self.when(cond, lambda: make().start())
         self.open.append((cond, lambda: make().wait_send()))
 
-    def copy(self, cond, src, dst):
-        slot = self.slot()
+    def copy(self, cond, src, dst, key=None):
+        slot = self.slot(key)
         make = lambda: pltpu.make_async_copy(view(src), view(dst), view(slot))
         self.when(cond, lambda: make().start())
         self.open.append((cond, lambda: make().wait()))
+
+    def block(self, cond, act):
+        inner = self.group()
+        self.when(cond, lambda: act(inner))
+        if inner.open:
+
+            def end():
+                for _, wait in inner.open:
+                    wait()
+
+            self.open.append((cond, end))
 
     @staticmethod
     def when(cond, act):
@@ -279,7 +294,7 @@
 def main_kernel(
     geo, w_hbm, xin, gin, cos_ref, sin_ref, so_ref, sa_ref, f_hbm, tail_ref,
     buf, hb, e_ref, vs, z_ref, x_ref, g_ref, v_ref,
-    vf, rowv, wq, wo, wu, wd, xh, n1, n2, qs, ks, vv, hid, du, ob, do, dqkv, dqs, acc, vp_ref, lse,
+    vf, rowv, wq, wo, wu, wd, xh, n1, n2, qs, ks, vv, hid, du, ob, do, dqkv, dqs, acc, vp_ref,
     rb_ref, rz, sibo, siba, rcvo, rcva, vr, vq, vsum, hbuf, lsem, ssem, rsem, csem, *spare,
 ):
     gz_ref = z_ref
@@ -291,34 +306,32 @@
     z, c = i // 2, i % 2
     sib = 2 * z + 1 - c
     near = (None, d - d % 2 + (1 - d % 2), (d + 2) % 4, 3 - d)
+    rank = [(d + k) % q for k in range(q)]
     dev = partial(geo.dev, rho=rho)
+    peers = [dev(e, i) for e in ((d, *near[1:]) if geo.square else rank)]
     early = Sends(ssem, rsem)
     tx = early.group()
     lc = Sends(csem, None)
     whole = slice(None)
 
-    def spread_one(tx, ok, part, sem):
+    def spread_one(tx, part, sem, key):
+        for k in (1, 2) if geo.square else range(1, q):
+            tx.send(None, part(d, None), part(d, None), sem + k - 1, peers[k], (key, 1, k))
+
+    def spread_two(tx, part, sem, key):
         if geo.square:
             for k in (1, 2):
-                tx.send(ok, part(d, None), part(d, None), sem + k - 1, dev(near[k], i))
+                arrive(part(near[k], None), (rsem, sem + k - 1))
+                half = part(near[k], k - 1)
+                tx.send(None, half, half, sem + 1 + k, peers[3 - k], (key, 2, k))
+
+    def spread_three(part, sem):
+        if geo.square:
+            for k in (1, 2):
+                arrive(part(near[3], k - 1), (rsem, sem + 1 + k))
         else:
             for k in range(1, q):
-                tx.send(ok, part(d, None), part(d, None), sem + k - 1, dev((d + k) % q, i))
-
-    def spread_two(tx, ok, part, sem):
-        if geo.square:
-            for k in (1, 2):
-                Sends.when(ok, lambda: arrive(part(near[k], None), (rsem, sem + k - 1)))
-                half = part(near[k], k - 1)
-                tx.send(ok, half, half, sem + 1 + k, dev(near[3 - k], i))
-
-    def spread_three(ok, part, sem):
-        if geo.square:
-            for k in (1, 2):
-                Sends.when(ok, lambda: arrive(part(near[3], k - 1), (rsem, sem + 1 + k)))
-        else:
-            for k in range(1, q):
-                Sends.when(ok, lambda: arrive(part((d + q - k) % q, None), (rsem, sem + k - 1)))
+                arrive(part(rank[q - k], None), (rsem, sem + k - 1))
 
     load = pltpu.make_async_copy(w_hbm, buf.at[pl.ds(HEAD, OWN)], lsem.at[0])
     load.start()
@@ -339,22 +352,29 @@
         early.send(z > 0, src, dst, 7 + 6 * a, dev(d, (i + V - 2) % V))
         early.send(None, src, dst, 2 + a, dev(d, sib))
 
-    def hop(a, ref, k):
+    def hop(a, ref, k, last):
         for s, sign in ((0, 1), (1, -1)):
             there = (z >= k + 1) if sign == 1 else (z + k + 1 < CHIPS)
+            on = (z < CHIPS - 1) if sign == 1 else (z > 0)
+            ok = there & jnp.logical_not(on) if last else there & on
             src_i = (i - 2 * sign * (k + 1) + 2 * V) % V
-            rows = pl.ds(mult(src_i * tl, 16), tl)
             rs = 4 + 6 * a + 3 * s + k
-            part = (ref, rows)
-
-            @pl.when(there)
+            part = (ref, pl.ds(mult(src_i * tl, 16), tl))
+
+            @pl.when(ok)
             def _():
                 arrive(part, (rsem, rs))
 
-            if k < CHIPS - 2:
-                on = (z < CHIPS - 1) if sign == 1 else (z > 0)
-                early.send(there & on, part, part, rs + 1, dev(d, (i + 2 * sign + V) % V))
-            early.send(there, part, part, 2 + a, dev(d, sib))
+            if not last:
+                early.send(ok, part, part, rs + 1, dev(d, (i + 2 * sign + V) % V))
+            early.send(ok, part, part, 2 + a, dev(d, sib), ("hop", a, k, s))
+
+    def relay(a, ref, k):
+        hop(a, ref, k, False)
+
+    def end_of_line(a, ref):
+        for k in range(CHIPS - 1):
+            hop(a, ref, k, True)
 
     chain(0, xin, x_ref)
     load.wait()
@@ -375,9 +395,9 @@
         tx = early.group()
         for cc in range(2):
             to = (2 * (z + k) + cc) % V
-            for ok, erow, zrow, n in owner_moves(geo, i, to):
+            for m, (ok, erow, zrow, n) in enumerate(owner_moves(geo, i, to)):
                 src = (e_ref, (to, d, pl.ds(erow, n)))
-                tx.send(ok, src, (z_ref, (d, pl.ds(zrow, n))), 16 + k, dev(d, to))
+                tx.send(ok, src, (z_ref, (d, pl.ds(zrow, n))), 16 + k, dev(d, to), ("slice", k, cc, m // 2))
         return tx
 
     def slices_of(k):
@@ -387,33 +407,32 @@
             at, n = (base, 2 * seg) if half is None else (base + half * seg, seg)
             return (z_ref, (e, pl.ds(mult(at, 16), n)))
 
-        return None, part, SPREAD + geo.ss * (k - 1)
+        return part, SPREAD + geo.ss * (k - 1), ("slices", k)
 
     first = slices_to(1)
     for k in range(1, V):
         early.send(i == V - 1, vs, v_ref, 1, dev(d, (i + k) % V))
-    for ok, erow, zrow, n in owner_moves(geo, i, sib):
+    for m, (ok, erow, zrow, n) in enumerate(owner_moves(geo, i, sib)):
         src = (e_ref, (sib, whole, pl.ds(erow, n)))
-        early.send(ok, src, (z_ref, (whole, pl.ds(zrow, n))), 16, dev(d, sib))
-    for ok, erow, zrow, n in owner_moves(geo, i, i):
-        lc.copy(ok, (e_ref, (i, whole, pl.ds(erow, n))), (z_ref, (whole, pl.ds(zrow, n))))
+        early.send(ok, src, (z_ref, (whole, pl.ds(zrow, n))), 16, dev(d, sib), ("slice", 0, 0, m // 2))
+    for m, (ok, erow, zrow, n) in enumerate(owner_moves(geo, i, i)):
+        lc.copy(ok, (e_ref, (i, whole, pl.ds(erow, n))), (z_ref, (whole, pl.ds(zrow, n))), ("own", m // 2))
     first.finish()
     second = slices_to(2)
+    relay(0, x_ref, 0)
     arrive((z_ref, (0, pl.ds(0, 2 * seg))), (rsem, 17))
     spread_one(early, *slices_of(1))
     second.finish()
     third = slices_to(3)
     arrive((z_ref, (0, pl.ds(0, 2 * seg))), (rsem, 18))
     spread_one(early, *slices_of(2))
-    third.finish()
-    hop(0, x_ref, 0)
+    relay(0, x_ref, 1)
+    chain(1, gin, g_ref)
     arrive((z_ref, (0, pl.ds(0, 2 * seg))), (rsem, 19))
     spread_one(early, *slices_of(3))
+    relay(1, g_ref, 0)
     spread_two(early, *slices_of(1))
-    hop(0, x_ref, 1)
-    chain(1, gin, g_ref)
     spread_two(early, *slices_of(2))
-    hop(0, x_ref, 2)
     for cp in own:
         cp.wait()
 
@@ -436,6 +455,7 @@
         return pl.ds(mult(r * RB, RB), RB)
 
     lane = lax.broadcasted_iota(jnp.int32, (RB, 128), 1)
+    end_of_line(0, x_ref)
     arrive((x_ref, pl.ds(0, CHIPS * tl)), (rsem, 2))
 
     def norms(r, carry):
@@ -452,17 +472,16 @@
         n2[rb, :] = (xhat * rowv[2:3, :] + rowv[3:4, :]).astype(BF16)
         return carry
 
+    spread_two(early, *slices_of(3))
     lax.fori_loop(0, nrb, norms, 0)
-    spread_two(early, *slices_of(3))
-    hop(1, g_ref, 0)
+    relay(1, g_ref, 1)
     sib_owner_rows(geo, sib, z_ref, (rsem, 16))
     lc.finish()
     for k in range(1, CHIPS):
-        spread_three(*slices_of(k))
+        spread_three(*slices_of(k)[:2])
     mats = (wq, wo, wu, wd)
     for e, zrow, n, m, row, ln in geo.maps():
         mats[m][row : row + n, ln : ln + 128] = z_ref[e, zrow : zrow + n, :]
-    hop(1, g_ref, 1)
 
     def forward(r, carry):
         rb = rb_of(r)
@@ -484,7 +503,6 @@
         return carry
 
     lax.fori_loop(0, nrb, forward, 0)
-    hop(1, g_ref, 2)
 
     ra = geo.rba
     left = lax.broadcasted_iota(jnp.int32, (ra, 128), 1) < 64
@@ -508,7 +526,7 @@
             top = jnp.max(s, axis=1, keepdims=True)
             ex = jnp.exp(s - top)
             tot = jnp.sum(ex, axis=1, keepdims=True)
-            lse[rb, h : h + 1] = top + jnp.log(tot)
+            xh[rb, 2 + h : 3 + h] = top + jnp.log(tot)
             outs.append(dot((ex * (1.0 / tot)).astype(BF16), vv[0:n, :]))
         ob[rb, :] = jnp.where(left, outs[0], outs[1]).astype(BF16)
 
@@ -522,34 +540,60 @@
             rows = pl.ds(mult((2 * k + 1 - c) * tl, 16), tl)
             tx.send(None, (part, rows), (sums, k), 20 + a, dev(d, sib))
 
-    def to_line(a, part, sums, got):
+    def line_rows(a, part, sums):
         arrive(sums, (rsem, 20 + a))
         for k in range(CHIPS):
             rows = pl.ds(mult((2 * k + c) * tl, 16), tl)
             sums[k] = (part[rows, :].astype(F32) + sums[k].astype(F32)).astype(BF16)
-        for k in range(1, CHIPS):
-            to = (z + k) % CHIPS
-            tx.send(None, (sums, to), (got, k - 1), 22 + a, dev(d, 2 * to + c))
+
+    def slot_of(s, step):
+        return 2 * (step - 1) - 1 + s if step > 1 else 0
+
+    def line_step(a, step, sums, got):
+        for s, sign in ((0, 1), (1, -1)):
+            far = z if sign == 1 else CHIPS - 1 - z
+            ok = far < step
+            dest = z + sign * (CHIPS - step)
+            rs = geo.lines + 6 * a + 3 * s + step - 1
+            if step > 1:
+
+                @pl.when(ok & (far > 0))
+                def _():
+                    at = slot_of(s, step - 1)
+                    arrive((got, at), (rsem, rs - 1))
+                    sums[dest] = (sums[dest].astype(F32) + got[at].astype(F32)).astype(BF16)
+
+            tx.send(ok, (sums, dest), (got, slot_of(s, step)), rs, dev(d, (i + 2 * sign + V) % V))
+
+    def line_end(a, sums, got, out):
+        tot = sums[z].astype(F32)
+        if a == 0:
+            tot = tot + (rowv[7:8, :] + rowv[8:9, :])
+        out[...] = tot
+        for s, more in ((0, z > 0), (1, z < CHIPS - 1)):
+
+            @pl.when(more)
+            def _():
+                at = slot_of(s, 3)
+                arrive((got, at), (rsem, geo.lines + 6 * a + 3 * s + 2))
+                out[...] += got[at].astype(F32)
 
     if not geo.tight:
         lax.fori_loop(0, nrb, outputs, 0)
         to_sibling(0, po_ref, sibo)
+    end_of_line(1, g_ref)
     arrive((g_ref, pl.ds(0, CHIPS * tl)), (rsem, 3))
 
-    def back_mlp(r, carry):
+    if not geo.tight:
+        line_rows(0, po_ref, sibo)
+        line_step(0, 1, sibo, rcvo)
+    def grad_heads(r, carry):
         rb = rb_of(r)
-        g = g_ref[rb, :]
-        dh = dot_nt(g, wd[...])
-        for b in range(4):
-            cols = slice(128 * b, 128 * b + 128)
-            low = (dh[:, cols] * buf[gp(b, r), :]).astype(BF16)
-            du[rb, cols] = low
-            acc[5:6, cols] += jnp.sum(low.astype(F32), axis=0, keepdims=True)
-        do[rb, :] = dot_nt(g, wo[...]).astype(BF16)
-        acc[4:5, :] += jnp.sum(g.astype(F32), axis=0, keepdims=True)
+        do[rb, :] = dot_nt(g_ref[rb, :], wo[...]).astype(BF16)
         return carry
 
-    lax.fori_loop(0, nrb, back_mlp, 0)
+    lax.fori_loop(0, nrb, grad_heads, 0)
+    third.finish()
     early.finish()
     pc = 4096 // q
     ph = pc // 2
@@ -565,24 +609,11 @@
                     gz_ref[e, pl.ds(mult(row + geo.ho * b, 16), geo.ho), :] = block
         return carry
 
-    def grad_cols(left_ref, right_ref, out, blocks):
-        def body(k, carry):
-            cols = pl.ds(mult(k * 256, 256), 256)
-            out[cols, :] = dot_tn(left_ref[:, cols], right_ref[...]).astype(BF16)
-            return carry
-
-        lax.fori_loop(0, blocks, body, 0)
-
-    def pack(which):
-        for e, zrow, n, m, row, ln in geo.maps():
-            if m in which:
-                gz_ref[e, zrow : zrow + n, :] = mats[m][row : row + n, ln : ln + 128]
-
     def halves(p, h):
         return pl.ds(p * pc + h * ph, ph), pl.ds(p * ph, ph)
 
     def sum_one(p):
-        sem = SUMS + geo.ss * p
+        sem = geo.sums + geo.ss * p
         if geo.square:
             for k in (1, 2):
                 rows, at = halves(p, k - 1)
@@ -596,7 +627,7 @@
                 tx.send(None, (gz_ref, (e, rows)), (rb_ref, (k - 1, rows)), sem + k - 1, dev(e, i))
 
     def sum_two(p):
-        sem = SUMS + geo.ss * p
+        sem = geo.sums + geo.ss * p
         if geo.square:
             for k in (1, 2):
                 rows, at = halves(p, k - 1)
@@ -607,7 +638,7 @@
                 tx.send(None, (rb_ref, (mid, at)), (rb_ref, (3 + k, at)), sem + 1 + k, dev(near[3 - k], i))
 
     def sum_three(p):
-        sem = SUMS + geo.ss * p
+        sem = geo.sums + geo.ss * p
         if geo.square:
             for k in (1, 2):
                 rows, at = halves(p, k - 1)
@@ -634,56 +665,58 @@
         ((5, 5 * seg + bp, bp, ap, 2), (6, 6 * seg, 0, ap, 2), (7, 6 * seg + 2 * ap, ap, ap, 2)),
     )
 
+    chip = [(z + k) % CHIPS for k in range(CHIPS)]
+    pair = [mult(2 * at, 2) for at in chip]
+    single = [(2 * at, 2 * at + 1) for at in chip]
+
     def to_owners(p):
         sum_three(p)
         for o, zrow, frow, n, kind in moves[p]:
             src, dst = (rz, pl.ds(zrow, n)), (fb, (i, d, pl.ds(frow, n)))
-            tx.send(i != o, src, dst, 27 + kind, dev(d, o))
-            lc.copy(i == o, src, dst)
+            tx.send(i != o, src, dst, PARTS + 4 * kind + (z + CHIPS - o // 2) % CHIPS, dev(d, o))
+            lc.copy(i == o, src, dst, ("part", kind))
         if p == 2:
             for o in (6, 7):
                 here = i // 4 == o - 6
                 src, dst = (rz, pl.ds(6 * seg + ap, ap)), (fb, (i, d, pl.ds(ap * (7 - o), ap)))
-                tx.send(here & (i != o), src, dst, 30, dev(d, o))
-                lc.copy(here & (i == o), src, dst)
-
-    def held(p):
-        out = [(o, 0, V, V - 1, frow, n, kind) for o, _, frow, n, kind in moves[p]]
+                rs = PARTS + 12 + (z + CHIPS - o // 2) % CHIPS
+                tx.send(here & (i != o), src, dst, rs, dev(d, o), ("last", 0))
+                lc.copy(here & (i == o), src, dst, ("part", 3))
+
+    def held(p, k):
+        out = [(o, frow, n, kind) for o, _, frow, n, kind in moves[p]]
         if p == 2:
-            out += [(6, 0, 4, 4, ap, ap, 3), (7, 4, 4, 3, 0, ap, 3)]
+            out += [(6, ap, ap, 3)] if k in (1, 2) else [(7, 0, ap, 3)]
         return out
 
-    def held_part(j0, js, frow, n):
-        def part(e, half):
-            at, m = (j0, js) if half is None else (j0 + half * (js // 2), js // 2)
-            return (fb, (pl.ds(at, m), e, pl.ds(frow, n)))
-
-        return part
-
-    def plane(p, stage):
-        if stage == 1:
+    def plane(p, stage, k):
+        if stage == 1 and k == 0:
             lc.finish()
-        for o, j0, js, remote, frow, n, kind in held(p):
-            ok, part, sem = i == o, held_part(j0, js, frow, n), SPREAD + geo.ss * (3 + kind)
-            if stage == 1:
-                Sends.when(ok, lambda: arrive((fb, (pl.ds(0, remote), 0, pl.ds(frow, n))), (rsem, 27 + kind)))
-                spread_one(tx, ok, part, sem)
-            elif stage == 2:
-                spread_two(tx, ok, part, sem)
-            else:
-                spread_three(ok, part, sem)
-
-    lax.fori_loop(0, 2, grad_down, 0)
-    sum_one(2)
-    if not geo.tight:
-        to_line(0, po_ref, sibo, rcvo)
+        for o, frow, n, kind in held(p, k):
+
+            def part(e, half):
+                js = pl.ds(pair[k], 2) if half is None else single[k][half]
+                return (fb, (js, e, pl.ds(frow, n)))
+
+            sem, key = SPREAD + geo.ss * (3 + 4 * kind + k), ("held", kind, k)
+
+            def act(tx):
+                if stage == 1:
+                    arrive((fb, (pl.ds(0, 2 if k else 1), 0, pl.ds(frow, n))), (rsem, PARTS + 4 * kind + k))
+                    spread_one(tx, part, sem, key)
+                elif stage == 2:
+                    spread_two(tx, part, sem, key)
+                else:
+                    spread_three(part, sem)
+
+            tx.block(i == o, act)
 
     for r in range(t // ra):
         rb, n = slice(r * ra, r * ra + ra), (r + 1) * ra
         dqh = []
         for h in range(2):
             qm, gm = mine(h, qs[rb, :]), mine(h, do[rb, :])
-            prob = jnp.exp(scores(r, qm) - lse[rb, h : h + 1])
+            prob = jnp.exp(scores(r, qm) - xh[rb, 2 + h : 3 + h])
             dp = dot_nt(gm, vv[0:n, :])
             delta = jnp.sum(prob * dp, axis=1, keepdims=True)
             ds = (prob * (dp - delta)).astype(BF16)
@@ -692,9 +725,10 @@
             buf[kv1 : kv1 + n, :] += dot_tn(prob.astype(BF16), gm)
         dqs[rb, :] = jnp.where(left, dqh[0], dqh[1])
 
-    sum_two(2)
-
-    def back(r, carry):
+    if not geo.tight:
+        line_step(0, 2, sibo, rcvo)
+
+    def back_one(r, carry):
         rb = rb_of(r)
         cos, sin = cos_ref[rb, :], sin_ref[rb, :]
         low = jnp.concatenate(
@@ -707,8 +741,41 @@
         )
         dqkv[rb, :] = low
         acc[6:7, 0:384] += jnp.sum(low.astype(F32), axis=0, keepdims=True)
+        return carry
+
+    lax.fori_loop(0, nrb, back_one, 0)
+    res = dot_tn(ob[...], g_ref[...]).astype(BF16)
+    for e in range(q):
+        for b in range(8):
+            row = 2 * seg + geo.ho * b
+            gz_ref[e, row : row + geo.ho, :] = res[geo.ho * e : geo.ho * e + geo.ho, 128 * b : 128 * b + 128]
+    for k in range(2):
+        res = dot_tn(n1[:, 512 * k : 512 * k + 512], dqkv[...]).astype(BF16)
+        for e in range(q):
+            for b in range(3):
+                row = seg * k + geo.qr * b
+                block = res[geo.qr * e : geo.qr * e + geo.qr, 128 * b : 128 * b + 128]
+                gz_ref[e, row : row + geo.qr, :] = block
+    sum_one(0)
+
+    def back_mlp(r, carry):
+        rb = rb_of(r)
+        g = g_ref[rb, :]
+        dh = dot_nt(g, wd[...])
+        for b in range(4):
+            cols = slice(128 * b, 128 * b + 128)
+            low = (dh[:, cols] * buf[gp(b, r), :]).astype(BF16)
+            du[rb, cols] = low
+            acc[5:6, cols] += jnp.sum(low.astype(F32), axis=0, keepdims=True)
+        acc[4:5, :] += jnp.sum(g.astype(F32), axis=0, keepdims=True)
+        return carry
+
+    lax.fori_loop(0, nrb, back_mlp, 0)
+
+    def back_two(r, carry):
+        rb = rb_of(r)
         xhat = (x_ref[rb, :].astype(F32) - xh[rb, 0:1]) * xh[rb, 1:2]
-        d1 = dot_nt(low, wq[...])
+        d1 = dot_nt(dqkv[rb, :], wq[...])
         acc[0:1, :] += jnp.sum(d1 * xhat, axis=0, keepdims=True)
         acc[1:2, :] += jnp.sum(d1, axis=0, keepdims=True)
         d2 = dot_nt(du[rb, :], wu[...])
@@ -717,28 +784,42 @@
         x_ref[rb, :] = (d1 * rowv[0:1, :] + d2 * rowv[2:3, :]).astype(BF16)
         return carry
 
-    lax.fori_loop(0, nrb, back, 0)
+    lax.fori_loop(0, nrb, back_two, 0)
     to_sibling(1, x_ref, siba)
-    res = dot_tn(ob[...], g_ref[...]).astype(BF16)
-    for e in range(q):
-        for b in range(8):
-            row = 2 * seg + geo.ho * b
-            gz_ref[e, row : row + geo.ho, :] = res[geo.ho * e : geo.ho * e + geo.ho, 128 * b : 128 * b + 128]
+    lax.fori_loop(0, 2, grad_down, 0)
+    sum_two(0)
+    sum_one(2)
     if geo.tight:
         lax.fori_loop(0, nrb, outputs, 0)
         to_sibling(0, po_ref, sibo)
-    grad_cols(n1, dqkv, wq, 4)
-    pack((0,))
-    sum_one(0)
+        line_rows(0, po_ref, sibo)
+        line_step(0, 1, sibo, rcvo)
+        line_step(0, 2, sibo, rcvo)
+    line_step(0, 3, sibo, rcvo)
+    line_rows(1, x_ref, siba)
+    line_step(1, 1, siba, rcva)
+    for r0, nr, off in geo.up_parts():
+        res = dot_tn(n2[:, r0 : r0 + q * nr], du[...]).astype(BF16)
+        for e in range(q):
+            for b in range(4):
+                gz_ref[e, off + nr * b : off + nr * b + nr, :] = res[nr * e : nr * e + nr, 128 * b : 128 * b + 128]
+    sum_one(1)
+    to_owners(0)
+    plane(0, 1, 0)
+    sum_two(2)
+    line_step(1, 2, siba, rcva)
     to_owners(2)
-    grad_cols(n2, du, wu, 4)
-    pack((2,))
-    sum_one(1)
-    sum_two(0)
-    if geo.tight:
-        to_line(0, po_ref, sibo, rcvo)
-    to_line(1, x_ref, siba, rcva)
-    plane(2, 1)
+    plane(2, 1, 0)
+    sum_two(1)
+    to_owners(1)
+    plane(1, 1, 0)
+    plane(0, 1, 1)
+    plane(0, 2, 0)
+    line_step(1, 3, siba, rcva)
+    plane(2, 1, 1)
+    plane(2, 2, 0)
+    plane(1, 1, 1)
+    plane(1, 2, 0)
     zeroth = jnp.where(j == 0, 1.0, 0.0)
     for b in range(8):
         cols = slice(128 * b, 128 * b + 128)
@@ -750,22 +831,15 @@
         vp_ref[pl.ds(32 + 8 * k + j, 1), :] = acc[6:7, 128 * k : 128 * k + 128]
     for k in range(4):
         vp_ref[pl.ds(72 + 8 * k + j, 1), :] = acc[5:6, 128 * k : 128 * k + 128]
-    tx.send(i < V - 1, vp_ref, (vr, i), 24, dev(d, V - 1))
-    to_owners(0)
-    sum_two(1)
-    plane(2, 2)
-    plane(0, 1)
-    to_owners(1)
-    plane(0, 2)
-    plane(1, 1)
-    for a, (sums, got, out) in enumerate(((sibo, rcvo, so_ref), (siba, rcva, sa_ref))):
-        arrive(got, (rsem, 22 + a))
-        tot = sums[z].astype(F32)
-        for k in range(CHIPS - 1):
-            tot = tot + got[k].astype(F32)
-        if a == 0:
-            tot = tot + (rowv[7:8, :] + rowv[8:9, :])
-        out[...] = tot
+    tx.send(i < V - 1, vp_ref, (vr, i), 26, dev(d, V - 1))
+    for k in (2, 3):
+        for p in (0, 2, 1):
+            plane(p, 1, k)
+            plane(p, 2, k - 1)
+    line_end(0, sibo, rcvo, so_ref)
+    line_end(1, siba, rcva, sa_ref)
+    for p in (0, 2, 1):
+        plane(p, 2, 3)
 
     def head_rows(jj, row, n, stride, s):
         for b in range(8):
@@ -791,23 +865,22 @@
 
     for e in range(q):
         to = dev(e, (i + V - 1) % V)
-        tx.send((d == 0) & (i > 0), (hbuf, pl.ds(0, VECS)), tail_ref, 26, to)
+        tx.send((d == 0) & (i > 0), (hbuf, pl.ds(0, VECS)), tail_ref, 28, to)
 
     @pl.when(i == V - 1)
     def _():
-        arrive((vr, pl.ds(0, V - 1)), (rsem, 24))
+        arrive((vr, pl.ds(0, V - 1)), (rsem, 26))
         tot = vp_ref[...]
         for k in range(V - 1):
             tot = tot + vr[k]
         vsum[...] = tot
 
     for k in range(1, q):
-        tx.send(i == V - 1, vsum, (vq, k - 1), 25, dev((d + k) % q, i))
-    plane(1, 2)
+        tx.send(i == V - 1, vsum, (vq, k - 1), 27, dev((d + k) % q, i))
 
     @pl.when(i == V - 1)
     def _():
-        arrive(vq, (rsem, 25))
+        arrive(vq, (rsem, 27))
         tot = vsum[...]
         for k in range(q - 1):
             tot = tot + vq[k]
@@ -815,10 +888,11 @@
 
     @pl.when(i < V - 1)
     def _():
-        arrive(tail_ref, (rsem, 26))
-
-    for p in (2, 0, 1):
-        plane(p, 3)
+        arrive(tail_ref, (rsem, 28))
+
+    for k in range(CHIPS):
+        for p in (0, 2, 1):
+            plane(p, 3, k)
     tx.finish()
     out = pltpu.make_async_copy(fb, f_hbm, lsem.at[3])
     out.start()
@@ -831,7 +905,7 @@
     hbm = pl.BlockSpec(memory_space=pl.ANY)
     cos, sin = rot_tables(t)
     line = pltpu.VMEM((CHIPS, tl, D), BF16)
-    line3 = pltpu.VMEM((CHIPS - 1, tl, D), BF16)
+    lines = pltpu.VMEM((2 * CHIPS - 3, tl, D), BF16)
     vec = pltpu.VMEM((VECS, 128), F32)
     low = lambda *dims: pltpu.VMEM(dims, BF16)
     full = lambda *dims: pltpu.VMEM(dims, F32)
@@ -860,7 +934,7 @@
             low(128, D),
             low(D, 512),
             low(512, D),
-            full(t, 2),
+            full(t, 4),
             low(t, D),
             low(t, D),
             low(t, 128),
@@ -874,36 +948,38 @@
             full(t, 128),
             full(8, D),
             vec,
-            full(t, 2),
             low(6, geo.zr // 2, 128) if geo.square else low(q - 1, geo.zr, 128),
             low(geo.zr, 128),
-            line, line, line3, line3,
+            line, line, lines, lines,
             full(V - 1, VECS, 128),
             full(q - 1, VECS, 128),
             vec,
             full(512, 128),
             pltpu.SemaphoreType.DMA((4,)),
-            pltpu.SemaphoreType.DMA((400,)),
-            pltpu.SemaphoreType.DMA((SUMS + 3 * geo.ss,)),
-            pltpu.SemaphoreType.DMA((24,)),
+            pltpu.SemaphoreType.DMA((184 if geo.square else 256,)),
+            pltpu.SemaphoreType.DMA((geo.lines + 12,)),
+            pltpu.SemaphoreType.DMA((8,)),
         ] + ([] if geo.tight else [low(t, D), low(V, q, geo.er, 128)]),
         compiler_params=pltpu.CompilerParams(
-            collective_id=0, has_side_effects=True, vmem_limit_bytes=63 << 20
+            collective_id=0, has_side_effects=True, vmem_limit_bytes=67_000_000
         ),
         name="layer",
     )(w, x, g, cos, sin)
 
 
 def adam_kernel(
-    geo, so_ref, sa_ref, x_ref, g_ref, tail_ref, f_hbm, w_hbm, m_hbm, s_hbm,
-    lo_ref, tg_ref, wg_hbm, nw_hbm, nm_hbm, ns_hbm, wb, mb, sb, ob, gb, fb, lsem,
+    geo, so_hbm, sa_hbm, x_hbm, g_hbm, tail_hbm, f_hbm, w_hbm, m_hbm, s_hbm,
+    lo_ref, tg_ref, wg_hbm, nw_hbm, nm_hbm, ns_hbm, wb, mb, sb, ob, gb, fb, so_ref, sa_ref, x_ref, g_ref, lsem,
 ):
     _, i, _ = geo.place()
-    loads = [pltpu.make_async_copy(f_hbm, fb, lsem.at[0])]
-    for k, (h, b) in enumerate(((w_hbm, wb), (m_hbm, mb), (s_hbm, sb))):
-        loads.append(pltpu.make_async_copy(h, b.at[pl.ds(0, OWN)], lsem.at[k + 1]))
+    first = (so_hbm, so_ref), (sa_hbm, sa_ref), (x_hbm, x_ref), (g_hbm, g_ref)
+    then = (tail_hbm, gb.at[pl.ds(ALI, VECS)]), (f_hbm, fb)
+    last = tuple((h, b.at[pl.ds(0, OWN)]) for h, b in ((w_hbm, wb), (m_hbm, mb), (s_hbm, sb)))
+    loads = [pltpu.make_async_copy(h, b, lsem.at[4 + k]) for k, (h, b) in enumerate(first + then + last)]
     for ld in loads:
         ld.start()
+    for ld in loads[:4]:
+        ld.wait()
     x = x_ref[...].astype(F32)
     sa = sa_ref[...]
     lo_ref[...] = (x + so_ref[...]).astype(BF16)
@@ -912,10 +988,10 @@
     xhat = mid * inv
     dx = inv * (sa - jnp.mean(sa, axis=1, keepdims=True) - xhat * jnp.mean(sa * xhat, axis=1, keepdims=True))
     tg_ref[...] = g_ref[...].astype(F32) + dx
-    gb[pl.ds(ALI, VECS), :] = tail_ref[...]
-    loads[0].wait()
+    for ld in loads[4:6]:
+        ld.wait()
     paste_share(geo, i, gb, fb)
-    for ld in loads[1:]:
+    for ld in loads[6:]:
         ld.wait()
     rows_n = 1024
     full = OWN // rows_n
@@ -925,7 +1001,7 @@
         rows = pl.ds(mult(n * rows_n, rows_n), rows_n)
         adam_rows(i, rows, n * rows_n, rows_n, wb, mb, sb, ob, gb)
         for k, (h, b) in enumerate(pairs):
-            pltpu.make_async_copy(b.at[rows], h.at[rows], lsem.at[4 + k]).start()
+            pltpu.make_async_copy(b.at[rows], h.at[rows], lsem.at[k]).start()
         return carry
 
     lax.fori_loop(0, full, adam, 0)
@@ -933,9 +1009,9 @@
     adam_rows(i, pl.ds(full * rows_n, 16), full * rows_n, 16, wb, mb, sb, ob, gb)
     for k, (h, b) in enumerate(pairs):
         rows = pl.ds(full * rows_n, rest)
-        pltpu.make_async_copy(b.at[rows], h.at[rows], lsem.at[4 + k]).start()
+        pltpu.make_async_copy(b.at[rows], h.at[rows], lsem.at[k]).start()
     for k, (h, b) in enumerate(pairs):
-        pltpu.make_async_copy(b.at[pl.ds(0, OWN)], h, lsem.at[4 + k]).wait()
+        pltpu.make_async_copy(b.at[pl.ds(0, OWN)], h, lsem.at[k]).wait()
 
 
 def adam_rows(i, rows, start, n, wb, mb, sb, ob, gb):
@@ -1025,15 +1101,19 @@
             jax.ShapeDtypeStruct((tl, D), F32),
             flat, flat, flat, flat,
         ),
-        in_specs=[vm] * 5 + [hbm] * 4,
+        in_specs=[hbm] * 9,
         out_specs=(vm, vm, hbm, hbm, hbm, hbm),
         scratch_shapes=[
             big, big, big, big,
             pltpu.VMEM((ALI + 128, 128), F32),
             pltpu.VMEM((V, geo.q, geo.er, 128), BF16),
-            pltpu.SemaphoreType.DMA((8,)),
+            pltpu.VMEM((tl, D), F32),
+            pltpu.VMEM((tl, D), F32),
+            pltpu.VMEM((tl, D), BF16),
+            pltpu.VMEM((tl, D), BF16),
+            pltpu.SemaphoreType.DMA((13,)),
         ],
-        compiler_params=pltpu.CompilerParams(vmem_limit_bytes=50 << 20),
+        compiler_params=pltpu.CompilerParams(vmem_limit_bytes=67_000_000),
         name="adam",
     )(so, sa, x, g, tail, f, w, m, s)
 

time: 186 us -> 165 us (0.89)
  Pallas kernels: 181 us -> 164 us
  local copies, waits for them, and re-layouts: 2.89 us -> 0 us
    pallas_call x1, Pallas kernels: 163 us -> 146 us  [main(): pl.pallas_call(partial(main_kernel, geo), out_shape=(jax.ShapeDtypeStruct...]
    unnamed x10 -> x0, local copies, waits for them, and re-layouts: 2.89 us -> none
where the time goes in v3:
time: 165 us
  Pallas kernels  164 us (99%)
    pallas_call x1, Pallas kernels, main(): pl.pallas_call(partial(main_kernel, geo), out_shape=(jax.ShapeDtypeStruct...  146 us
    pallas_call x1, Pallas kernels, adam(): pl.pallas_call(partial(adam_kernel, geo), out_shape=(jax.ShapeDtypeStruct...  18.7 us

profile of v3, /device:TPU:15, one launch (start us, length us, event | category | flops | bytes accessed | tf_op | source)
XLA Modules:
  0.0 165.3 jit_solution(17509612698644755220)
XLA Ops:
  0.6 145.7 %layer.1 = (f32[128,1024]{1,0:T(8,128)}, f32[128,1024]{1,0:T(8,128)}, bf16[8,4,512,128]{3,2,1,0:T(8,128)(2,1)}, f32[104,128]{1,0:T(8,128)}) custom-call(f32[12301,128]{1,0:T(8,128)} %bitcast.11, bf16[128,1024]{1,0:T(8,128)(2,1)} %bitcast.15, bf16[128,1024]{1,0:T(8,128)(2,1)} %bitcast.17, f32[1024,128]{1,0:T(8,128)} %constant.4.clone.cos_ref, ...), custom_call_target="tpu_custom_call" | custom-call | tf_op jit(solution)/shard_map/layer/pallas_call | solution.py:912
  146.4 18.7 %adam.1 = (bf16[128,1024]{1,0:T(8,128)(2,1)}, f32[128,1024]{1,0:T(8,128)}, f32[12301,128]{1,0:T(8,128)}, f32[12301,128]{1,0:T(8,128)}, f32[12301,128]{1,0:T(8,128)}, /*index=5*/f32[12301,128]{1,0:T(8,128)}) custom-call(f32[128,1024]{1,0:T(8,128)} %get-tuple-element.16.so_hbm, f32[128,1024]{1,0:T(8,128)} %get-tuple-element.17.sa_hbm, ...), custom_call_target="tpu_custom_call" | custom-call | tf_op jit(solution)/shard_map/adam/pallas_call | solution.py:1097

commit v4 on v3

--- a/solution.py
+++ b/solution.py
@@ -32,7 +32,7 @@
 HEAD = 112
 RB = 256
 PARTS = 29
-SPREAD = 45
+SPREAD = 37
 
 
 class Geo:
@@ -55,7 +55,7 @@
         self.rba = RB // 2 if self.tight else RB
         self.square = q == 4
         self.ss = max(4, q - 1)
-        self.sums = SPREAD + 19 * self.ss
+        self.sums = SPREAD + 11 * self.ss
         self.lines = self.sums + 3 * self.ss
 
     def place(self):
@@ -593,6 +593,21 @@
         return carry
 
     lax.fori_loop(0, nrb, grad_heads, 0)
+
+    def back_mlp(r, carry):
+        rb = rb_of(r)
+        g = g_ref[rb, :]
+        dh = dot_nt(g, wd[...])
+        for b in range(4):
+            cols = slice(128 * b, 128 * b + 128)
+            low = (dh[:, cols] * buf[gp(b, r), :]).astype(BF16)
+            du[rb, cols] = low
+            acc[5:6, cols] += jnp.sum(low.astype(F32), axis=0, keepdims=True)
+        acc[4:5, :] += jnp.sum(g.astype(F32), axis=0, keepdims=True)
+        return carry
+
+    lax.fori_loop(0, nrb, back_mlp, 0)
+
     third.finish()
     early.finish()
     pc = 4096 // q
@@ -673,13 +688,13 @@
         sum_three(p)
         for o, zrow, frow, n, kind in moves[p]:
             src, dst = (rz, pl.ds(zrow, n)), (fb, (i, d, pl.ds(frow, n)))
-            tx.send(i != o, src, dst, PARTS + 4 * kind + (z + CHIPS - o // 2) % CHIPS, dev(d, o))
+            tx.send(i != o, src, dst, PARTS + 4 * (kind % 2) + (z + CHIPS - o // 2) % CHIPS, dev(d, o))
             lc.copy(i == o, src, dst, ("part", kind))
         if p == 2:
             for o in (6, 7):
                 here = i // 4 == o - 6
                 src, dst = (rz, pl.ds(6 * seg + ap, ap)), (fb, (i, d, pl.ds(ap * (7 - o), ap)))
-                rs = PARTS + 12 + (z + CHIPS - o // 2) % CHIPS
+                rs = PARTS + 4 + (z + CHIPS - o // 2) % CHIPS
                 tx.send(here & (i != o), src, dst, rs, dev(d, o), ("last", 0))
                 lc.copy(here & (i == o), src, dst, ("part", 3))
 
@@ -698,11 +713,11 @@
                 js = pl.ds(pair[k], 2) if half is None else single[k][half]
                 return (fb, (js, e, pl.ds(frow, n)))
 
-            sem, key = SPREAD + geo.ss * (3 + 4 * kind + k), ("held", kind, k)
+            sem, key = SPREAD + geo.ss * (3 + 4 * (kind % 2) + k), ("held", kind % 2, k)
 
             def act(tx):
                 if stage == 1:
-                    arrive((fb, (pl.ds(0, 2 if k else 1), 0, pl.ds(frow, n))), (rsem, PARTS + 4 * kind + k))
+                    arrive((fb, (pl.ds(0, 2 if k else 1), 0, pl.ds(frow, n))), (rsem, PARTS + 4 * (kind % 2) + k))
                     spread_one(tx, part, sem, key)
                 elif stage == 2:
                     spread_two(tx, part, sem, key)
@@ -710,6 +725,9 @@
                     spread_three(part, sem)
 
             tx.block(i == o, act)
+
+    lax.fori_loop(0, 2, grad_down, 0)
+    sum_one(2)
 
     for r in range(t // ra):
         rb, n = slice(r * ra, r * ra + ra), (r + 1) * ra
@@ -725,6 +743,7 @@
             buf[kv1 : kv1 + n, :] += dot_tn(prob.astype(BF16), gm)
         dqs[rb, :] = jnp.where(left, dqh[0], dqh[1])
 
+    sum_two(2)
     if not geo.tight:
         line_step(0, 2, sibo, rcvo)
 
@@ -757,20 +776,10 @@
                 block = res[geo.qr * e : geo.qr * e + geo.qr, 128 * b : 128 * b + 128]
                 gz_ref[e, row : row + geo.qr, :] = block
     sum_one(0)
-
-    def back_mlp(r, carry):
-        rb = rb_of(r)
-        g = g_ref[rb, :]
-        dh = dot_nt(g, wd[...])
-        for b in range(4):
-            cols = slice(128 * b, 128 * b + 128)
-            low = (dh[:, cols] * buf[gp(b, r), :]).astype(BF16)
-            du[rb, cols] = low
-            acc[5:6, cols] += jnp.sum(low.astype(F32), axis=0, keepdims=True)
-        acc[4:5, :] += jnp.sum(g.astype(F32), axis=0, keepdims=True)
-        return carry
-
-    lax.fori_loop(0, nrb, back_mlp, 0)
+    to_owners(2)
+    plane(2, 1, 0)
+    if not geo.tight:
+        line_step(0, 3, sibo, rcvo)
 
     def back_two(r, carry):
         rb = rb_of(r)
@@ -786,38 +795,32 @@
 
     lax.fori_loop(0, nrb, back_two, 0)
     to_sibling(1, x_ref, siba)
-    lax.fori_loop(0, 2, grad_down, 0)
+    for r0, nr, off in geo.up_parts():
+        res = dot_tn(n2[:, r0 : r0 + q * nr], du[...]).astype(BF16)
+        for e in range(q):
+            for b in range(4):
+                gz_ref[e, off + nr * b : off + nr * b + nr, :] = res[nr * e : nr * e + nr, 128 * b : 128 * b + 128]
     sum_two(0)
-    sum_one(2)
+    sum_one(1)
     if geo.tight:
         lax.fori_loop(0, nrb, outputs, 0)
         to_sibling(0, po_ref, sibo)
         line_rows(0, po_ref, sibo)
         line_step(0, 1, sibo, rcvo)
         line_step(0, 2, sibo, rcvo)
-    line_step(0, 3, sibo, rcvo)
+        line_step(0, 3, sibo, rcvo)
     line_rows(1, x_ref, siba)
     line_step(1, 1, siba, rcva)
-    for r0, nr, off in geo.up_parts():
-        res = dot_tn(n2[:, r0 : r0 + q * nr], du[...]).astype(BF16)
-        for e in range(q):
-            for b in range(4):
-                gz_ref[e, off + nr * b : off + nr * b + nr, :] = res[nr * e : nr * e + nr, 128 * b : 128 * b + 128]
-    sum_one(1)
     to_owners(0)
     plane(0, 1, 0)
-    sum_two(2)
+    sum_two(1)
+    plane(2, 1, 1)
+    plane(2, 2, 0)
+    to_owners(1)
     line_step(1, 2, siba, rcva)
-    to_owners(2)
-    plane(2, 1, 0)
-    sum_two(1)
-    to_owners(1)
     plane(1, 1, 0)
     plane(0, 1, 1)
     plane(0, 2, 0)
-    line_step(1, 3, siba, rcva)
-    plane(2, 1, 1)
-    plane(2, 2, 0)
     plane(1, 1, 1)
     plane(1, 2, 0)
     zeroth = jnp.where(j == 0, 1.0, 0.0)
@@ -833,9 +836,11 @@
         vp_ref[pl.ds(72 + 8 * k + j, 1), :] = acc[5:6, 128 * k : 128 * k + 128]
     tx.send(i < V - 1, vp_ref, (vr, i), 26, dev(d, V - 1))
     for k in (2, 3):
-        for p in (0, 2, 1):
+        for p in (2, 0, 1):
             plane(p, 1, k)
             plane(p, 2, k - 1)
+        if k == 2:
+            line_step(1, 3, siba, rcva)
     line_end(0, sibo, rcvo, so_ref)
     line_end(1, siba, rcva, sa_ref)
     for p in (0, 2, 1):
@@ -893,10 +898,10 @@
     for k in range(CHIPS):
         for p in (0, 2, 1):
             plane(p, 3, k)
+        js = pl.ds(pair[k], 2)
+        lc.copy(None, (fb, js), (f_hbm, js), ("part", k))
     tx.finish()
-    out = pltpu.make_async_copy(fb, f_hbm, lsem.at[3])
-    out.start()
-    out.wait()
+    lc.finish()
 
 
 def main(geo, w, x, g):
@@ -956,7 +961,7 @@
             vec,
             full(512, 128),
             pltpu.SemaphoreType.DMA((4,)),
-            pltpu.SemaphoreType.DMA((184 if geo.square else 256,)),
+            pltpu.SemaphoreType.DMA((150 if geo.square else 256,)),
             pltpu.SemaphoreType.DMA((geo.lines + 12,)),
             pltpu.SemaphoreType.DMA((8,)),
         ] + ([] if geo.tight else [low(t, D), low(V, q, geo.er, 128)]),

time: 165 us -> 160 us (0.970)
  Pallas kernels: 164 us -> 159 us
    pallas_call x1, Pallas kernels: 146 us -> 140 us  [main(): pl.pallas_call(partial(main_kernel, geo), out_shape=(jax.ShapeDtypeStruct...]
where the time goes in v4:
time: 160 us; the launch traced here: 159 us
  Pallas kernels  159 us (99%)
    pallas_call x1, Pallas kernels, main(): pl.pallas_call(partial(main_kernel, geo), out_shape=(jax.ShapeDtypeStruct...  140 us
    pallas_call x1, Pallas kernels, adam(): pl.pallas_call(partial(adam_kernel, geo), out_shape=(jax.ShapeDtypeStruct...  18.7 us

profile of v4, /device:TPU:15, one launch (start us, length us, event | category | flops | bytes accessed | tf_op | source)
XLA Modules:
  0.0 159.4 jit_solution(13657123917367519700)
XLA Ops:
  0.6 139.8 %layer.1 = (f32[128,1024]{1,0:T(8,128)}, f32[128,1024]{1,0:T(8,128)}, bf16[8,4,512,128]{3,2,1,0:T(8,128)(2,1)}, f32[104,128]{1,0:T(8,128)}) custom-call(f32[12301,128]{1,0:T(8,128)} %bitcast.11, bf16[128,1024]{1,0:T(8,128)(2,1)} %bitcast.15, bf16[128,1024]{1,0:T(8,128)(2,1)} %bitcast.17, f32[1024,128]{1,0:T(8,128)} %constant.4.clone.cos_ref, ...), custom_call_target="tpu_custom_call" | custom-call | tf_op jit(solution)/shard_map/layer/pallas_call | solution.py:917
  140.5 18.7 %adam.1 = (bf16[128,1024]{1,0:T(8,128)(2,1)}, f32[128,1024]{1,0:T(8,128)}, f32[12301,128]{1,0:T(8,128)}, f32[12301,128]{1,0:T(8,128)}, f32[12301,128]{1,0:T(8,128)}, /*index=5*/f32[12301,128]{1,0:T(8,128)}) custom-call(f32[128,1024]{1,0:T(8,128)} %get-tuple-element.16.so_hbm, f32[128,1024]{1,0:T(8,128)} %get-tuple-element.17.sa_hbm, ...), custom_call_target="tpu_custom_call" | custom-call | tf_op jit(solution)/shard_map/adam/pallas_call | solution.py:1102

commit v5 on v4

--- a/solution.py
+++ b/solution.py
@@ -292,7 +292,8 @@
 
 
 def main_kernel(
-    geo, w_hbm, xin, gin, cos_ref, sin_ref, so_ref, sa_ref, f_hbm, tail_ref,
+    geo, w_hbm, xin, gin, cos_hbm, sin_hbm, so_hbm, sa_hbm, f_hbm, tail_ref,
+    cos_ref, sin_ref, so_ref, sa_ref,
     buf, hb, e_ref, vs, z_ref, x_ref, g_ref, v_ref,
     vf, rowv, wq, wo, wu, wd, xh, n1, n2, qs, ks, vv, hid, du, ob, do, dqkv, dqs, acc, vp_ref,
     rb_ref, rz, sibo, siba, rcvo, rcva, vr, vq, vsum, hbuf, lsem, ssem, rsem, csem, *spare,
@@ -309,8 +310,8 @@
     rank = [(d + k) % q for k in range(q)]
     dev = partial(geo.dev, rho=rho)
     peers = [dev(e, i) for e in ((d, *near[1:]) if geo.square else rank)]
-    early = Sends(ssem, rsem)
-    tx = early.group()
+    early = Sends(ssem, rsem, dict.fromkeys(range(8)))
+    tx = Sends(ssem, rsem)
     lc = Sends(csem, None)
     whole = slice(None)
 
@@ -339,6 +340,8 @@
     own = [
         pltpu.make_async_copy(xin, x_ref.at[rows_own], lsem.at[1]),
         pltpu.make_async_copy(gin, g_ref.at[rows_own], lsem.at[2]),
+        pltpu.make_async_copy(cos_hbm, cos_ref, lsem.at[3]),
+        pltpu.make_async_copy(sin_hbm, sin_ref, lsem.at[4]),
     ]
     for cp in own:
         cp.start()
@@ -843,6 +846,8 @@
             line_step(1, 3, siba, rcva)
     line_end(0, sibo, rcvo, so_ref)
     line_end(1, siba, rcva, sa_ref)
+    lc.copy(None, so_ref, so_hbm, ("out", 0))
+    lc.copy(None, sa_ref, sa_hbm, ("out", 1))
     for p in (0, 2, 1):
         plane(p, 2, 3)
 
@@ -922,9 +927,13 @@
             jax.ShapeDtypeStruct((V, q, geo.er, 128), BF16),
             jax.ShapeDtypeStruct((VECS, 128), F32),
         ),
-        in_specs=[hbm, hbm, hbm, vm, vm],
-        out_specs=(vm, vm, hbm, vm),
+        in_specs=[hbm] * 5,
+        out_specs=(hbm, hbm, hbm, vm),
         scratch_shapes=[
+            full(t, 128),
+            full(t, 128),
+            full(tl, D),
+            full(tl, D),
             full(HEAD + OWN + 3, 128),
             full(112, 128),
             low(V, q, geo.er, 128),
@@ -960,8 +969,8 @@
             full(q - 1, VECS, 128),
             vec,
             full(512, 128),
-            pltpu.SemaphoreType.DMA((4,)),
-            pltpu.SemaphoreType.DMA((150 if geo.square else 256,)),
+            pltpu.SemaphoreType.DMA((5,)),
+            pltpu.SemaphoreType.DMA((92 if geo.square else 256,)),
             pltpu.SemaphoreType.DMA((geo.lines + 12,)),
             pltpu.SemaphoreType.DMA((8,)),
         ] + ([] if geo.tight else [low(t, D), low(V, q, geo.er, 128)]),
@@ -979,9 +988,16 @@
     _, i, _ = geo.place()
     first = (so_hbm, so_ref), (sa_hbm, sa_ref), (x_hbm, x_ref), (g_hbm, g_ref)
     then = (tail_hbm, gb.at[pl.ds(ALI, VECS)]), (f_hbm, fb)
-    last = tuple((h, b.at[pl.ds(0, OWN)]) for h, b in ((w_hbm, wb), (m_hbm, mb), (s_hbm, sb)))
-    loads = [pltpu.make_async_copy(h, b, lsem.at[4 + k]) for k, (h, b) in enumerate(first + then + last)]
-    for ld in loads:
+    loads = [pltpu.make_async_copy(h, b, lsem.at[4 + k]) for k, (h, b) in enumerate(first + then)]
+    cuts = [4096 * k for k in range(OWN // 4096 + 1)] + [OWN]
+    parts = [
+        [
+            pltpu.make_async_copy(h.at[pl.ds(lo, hi - lo)], b.at[pl.ds(lo, hi - lo)], lsem.at[10 + 3 * n + k])
+            for k, (h, b) in enumerate(((w_hbm, wb), (m_hbm, mb), (s_hbm, sb)))
+        ]
+        for n, (lo, hi) in enumerate(zip(cuts, cuts[1:]))
+    ]
+    for ld in loads + sum(parts, []):
         ld.start()
     for ld in loads[:4]:
         ld.wait()
@@ -996,8 +1012,6 @@
     for ld in loads[4:6]:
         ld.wait()
     paste_share(geo, i, gb, fb)
-    for ld in loads[6:]:
-        ld.wait()
     rows_n = 1024
     full = OWN // rows_n
     pairs = ((wg_hbm, ob), (nw_hbm, wb), (nm_hbm, mb), (ns_hbm, sb))
@@ -1009,7 +1023,10 @@
             pltpu.make_async_copy(b.at[rows], h.at[rows], lsem.at[k]).start()
         return carry
 
-    lax.fori_loop(0, full, adam, 0)
+    for n, part in enumerate(parts):
+        for ld in part:
+            ld.wait()
+        lax.fori_loop(min(4 * n, full), min(4 * n + 4, full), adam, 0)
     rest = OWN - full * rows_n
     adam_rows(i, pl.ds(full * rows_n, 16), full * rows_n, 16, wb, mb, sb, ob, gb)
     for k, (h, b) in enumerate(pairs):
@@ -1116,7 +1133,7 @@
             pltpu.VMEM((tl, D), F32),
             pltpu.VMEM((tl, D), BF16),
             pltpu.VMEM((tl, D), BF16),
-            pltpu.SemaphoreType.DMA((13,)),
+            pltpu.SemaphoreType.DMA((24,)),
         ],
         compiler_params=pltpu.CompilerParams(vmem_limit_bytes=67_000_000),
         name="adam",

time: 160 us -> 158 us (0.988)
  Pallas kernels: 159 us -> 157 us
    pallas_call x1, Pallas kernels: 140 us -> 138 us  [main(): pl.pallas_call(partial(main_kernel, geo), out_shape=(jax.ShapeDtypeStruct...]
where the time goes in v5:
time: 158 us
  Pallas kernels  157 us (99%)
    pallas_call x1, Pallas kernels, main(): pl.pallas_call(partial(main_kernel, geo), out_shape=(jax.ShapeDtypeStruct...  138 us
    pallas_call x1, Pallas kernels, adam(): pl.pallas_call(partial(adam_kernel, geo), out_shape=(jax.ShapeDtypeStruct...  18.8 us

profile of v5, /device:TPU:15, one launch (start us, length us, event | category | flops | bytes accessed | tf_op | source)
XLA Modules:
  0.0 157.6 jit_solution(10772954893278149643)
XLA Ops:
  0.6 137.9 %layer.1 = (f32[128,1024]{1,0:T(8,128)}, f32[128,1024]{1,0:T(8,128)}, bf16[8,4,512,128]{3,2,1,0:T(8,128)(2,1)}, f32[104,128]{1,0:T(8,128)}) custom-call(f32[12301,128]{1,0:T(8,128)} %bitcast.11, bf16[128,1024]{1,0:T(8,128)(2,1)} %bitcast.15, bf16[128,1024]{1,0:T(8,128)(2,1)} %bitcast.17, f32[1024,128]{1,0:T(8,128)} %constant.4.clone.cos_hbm, ...), custom_call_target="tpu_custom_call" | custom-call | tf_op jit(solution)/shard_map/layer/pallas_call | solution.py:922
  138.6 18.8 %adam.1 = (bf16[128,1024]{1,0:T(8,128)(2,1)}, f32[128,1024]{1,0:T(8,128)}, f32[12301,128]{1,0:T(8,128)}, f32[12301,128]{1,0:T(8,128)}, f32[12301,128]{1,0:T(8,128)}, /*index=5*/f32[12301,128]{1,0:T(8,128)}) custom-call(f32[128,1024]{1,0:T(8,128)} %get-tuple-element.16.so_hbm, f32[128,1024]{1,0:T(8,128)} %get-tuple-element.17.sa_hbm, ...), custom_call_target="tpu_custom_call" | custom-call | tf_op jit(solution)/shard_map/adam/pallas_call | solution.py:1119
